TPU v7x, 32 devices: a whole 2x2x4 slice. The times are simulated.
32 devices in a mesh: partner: 8 (over y, x, core), block: 4 (over z).
Axes of the slice: x: 2, y: 2, z: 4, core: 2. Of those that a mesh axis runs over, the one named last changes fastest.
Arguments:
- points: bfloat16 [32, 32768], P(None, ('partner', 'block')), may hold values from -6 to 6
- tree_order: int32 [32768], P(('partner', 'block')), may hold values from 0 to 32767, as said below
- nearby_dense_blocks: bfloat16 [256, 3, 128, 128], P(('partner', 'block')), may hold values from -0.3125 to 0.3125
- neighbours: int32 [256, 3], P(('partner', 'block')), may hold values from 0 to 255, as said below
- compress: bfloat16 [256, 128, 128], P(('partner', 'block')), may hold values from -0.5 to 0.5
- expand: bfloat16 [256, 128, 128], P(('partner', 'block')), may hold values from -0.5 to 0.5
- top_factor: bfloat16 [256, 128, 128], P(('partner', 'block')), may hold values from -0.5 to 0.5
- butterfly_mixers: bfloat16 [2, 256, 2, 128, 128], P(None, ('partner', 'block')), may hold values from -0.375 to 0.375
- block_map: int32 [3, 8], replicated, may hold values from 0 to 7, as said below
Outputs:
- applied: bfloat16 [32, 32768], P(None, ('partner', 'block'))
Inputs may be any that keep to these rules, and one draw needn't show every extreme that they name: tree_order[r] lies among the 1024 points of the aligned group of 1024 rows that holds r, and names every point once. neighbours[l, 0] is l; every other entry lies within 2 leaves of l and in the same aligned group of 32 leaves as l. `block_map`: each row names exactly 4 different slots, each of them twice.
All inputs are finite; a program needn't handle non-finite values.
Results may differ from a plain program's by a relative error of at most 0.001.
Values may be sent and summed in bfloat16 or wider, within the bound.
No kernel may reach another device: no remote copies, remote signals or barrier semaphores. Data moves between devices by JAX's collectives and lax.ppermute only.
A program may use at most 64 MiB of HBM per device.

v0:
```python
import functools

import jax
import jax.numpy as jnp
from jax import lax
from jax.experimental import pallas as pl
from jax.experimental.pallas import tpu as pltpu
from jax.sharding import PartitionSpec as P


REACH = 2
LANES = 128
VMEM = pl.BlockSpec(memory_space=pltpu.VMEM)
HBM = pl.BlockSpec(memory_space=pltpu.HBM)


def call(body, outs, in_specs, scratch=(), flops=1 << 20, moved=1 << 18, place=VMEM):
    single = not isinstance(outs, (list, tuple))
    run = pl.pallas_call(
        body,
        out_shape=outs,
        in_specs=in_specs,
        out_specs=place if single else [VMEM] * len(outs),
        scratch_shapes=list(scratch),
        compiler_params=pltpu.CompilerParams(vmem_limit_bytes=16 << 20),
        cost_estimate=pl.CostEstimate(flops=flops, bytes_accessed=moved, transcendentals=0),
    )

    def bound(*args):
        return run(
            *[
                pltpu.with_memory_space_constraint(a, pltpu.HBM) if s is HBM else a
                for a, s in zip(args, in_specs)
            ]
        )

    return bound


def tables(map_ref, row, slot_ref, rank_ref, slots):
    mask = jnp.int32(0)
    for i in range(slots):
        mask = mask | (jnp.int32(1) << map_ref[row, i])
    rank = jnp.int32(0)
    for j in range(slots):
        slot_ref[rank] = jnp.int32(j)
        rank_ref[j] = rank
        rank = rank + ((mask >> j) & 1)


class Places:
    def __init__(self, levels, leaves, near_count):
        self.leaves, self.half = leaves, leaves // 2
        self.level_rows = leaves + 2 * self.half
        self.near_base = levels * self.level_rows
        self.near_count = near_count
        self.rows = -(-(self.near_base + leaves * near_count) // 8) * 8

    def piece(self, level, i):
        return level * self.level_rows + i

    def slot(self, level, k):
        return level * self.level_rows + self.leaves + k

    def slot_piece(self, level, k):
        return level * self.level_rows + self.leaves + self.half + k

    def near(self, leaf, n):
        return self.near_base + leaf * self.near_count + n


def read(table, row):
    return table[pl.ds(row, 1), :][0, 0]


def split(x):
    high = x.astype(jnp.bfloat16)
    low = (x - high.astype(jnp.float32)).astype(jnp.bfloat16)
    return jnp.concatenate([high, low], axis=0)


def times(pair, factor):
    both = jnp.dot(pair, factor, preferred_element_type=jnp.float32)
    rows = both.shape[0] // 2
    return both[:rows] + both[rows:]


def pick_lanes(blocks, high, low):
    rows = blocks[0].shape[0]
    high = jnp.broadcast_to(high, (rows, LANES))
    low = jnp.broadcast_to(low, (rows, LANES))
    out = jnp.take_along_axis(blocks[0], low, axis=1)
    for b in range(1, len(blocks)):
        out = jnp.where(high == b, jnp.take_along_axis(blocks[b], low, axis=1), out)
    return out


def column_blocks(x, leaves):
    return [x[:, b * LANES : (b + 1) * LANES].astype(jnp.float32) for b in range(leaves)]


def first_body(points, order, compress, block_map, sent, pts, idx, comp, table, slot, rank, sems):
    leaves = idx.shape[0]
    copies = [
        pltpu.make_async_copy(block_map, table, sems.at[0]),
        pltpu.make_async_copy(order, idx, sems.at[1]),
        pltpu.make_async_copy(points, pts, sems.at[2]),
        pltpu.make_async_copy(compress, comp, sems.at[3]),
    ]
    for copy in copies:
        copy.start()
    copies[0].wait()
    tables(table, 0, slot, rank, leaves)
    copies[1].wait()
    copies[2].wait()
    blocks = column_blocks(pts[...], leaves)
    rows = []
    for k in range(leaves // 2):
        local = idx[pl.ds(slot[k], 1), :] & (leaves * LANES - 1)
        rows.append(pick_lanes(blocks, local >> 7, local & (LANES - 1)).astype(jnp.bfloat16))
    copies[3].wait()
    for k in range(leaves // 2):
        sent[k] = split(jnp.dot(rows[k], comp[slot[k]], preferred_element_type=jnp.float32))


def order_body(
    places, points, order, block_map, near, mixers, dense, expand,
    ordered, even, odd, table, mixers_out, dense_out, expand_out, maps, nears, slot, rank, sems,
):
    leaves = order.shape[0]
    levels = maps.shape[0]
    copies = [
        pltpu.make_async_copy(block_map, maps, sems.at[0]),
        pltpu.make_async_copy(near, nears, sems.at[1]),
        pltpu.make_async_copy(mixers, mixers_out, sems.at[2]),
        pltpu.make_async_copy(dense, dense_out, sems.at[3]),
        pltpu.make_async_copy(expand, expand_out, sems.at[4]),
    ]
    for copy in copies:
        copy.start()
    blocks = column_blocks(points[...], leaves)
    for leaf in range(leaves):
        local = order[pl.ds(leaf, 1), :] & (leaves * LANES - 1)
        ordered[leaf] = pick_lanes(blocks, local >> 7, local & (LANES - 1)).astype(jnp.bfloat16)
    block = lax.axis_index("block")
    parity = block & 1
    head, tail = 0, leaves - REACH
    even[...] = ordered[pl.ds(jnp.where(parity == 0, tail, head), REACH)]
    odd[...] = ordered[pl.ds(jnp.where(parity == 0, head, tail), REACH)]
    base = (lax.axis_index("partner") * lax.axis_size("block") + block) * leaves

    def put(row, value):
        table[pl.ds(row, 1), :] = jnp.full((1, LANES), value, jnp.int32)

    copies[0].wait()
    copies[1].wait()
    for level in range(levels):
        tables(maps, level, slot, rank, leaves)
        for i in range(leaves):
            put(places.piece(level, i), rank[maps[level, i]])
        if level > 0:
            for k in range(leaves // 2):
                i = slot[k]
                put(places.slot(level, k), i)
                put(places.slot_piece(level, k), read(table, places.piece(level - 1, i)))
    for leaf in range(leaves):
        for n in range(nears.shape[0]):
            put(places.near(leaf, n), nears[n, leaf] - base + REACH)
    for copy in copies[2:]:
        copy.wait()


def prep_body(order, mixers, expand, place, joint_own, joint):
    leaves = order.shape[0]
    count = leaves * LANES
    target = lax.broadcasted_iota(jnp.int32, (count, LANES), 0)
    kind = lax.broadcasted_iota(jnp.int32, (8, LANES), 0)
    lane = lax.broadcasted_iota(jnp.int32, (8, LANES), 1)
    total = None
    for leaf in range(leaves):
        local = order[pl.ds(leaf, 1), :] & (count - 1)
        hit = jnp.where(target == local, 1.0, 0.0).astype(jnp.bfloat16)
        value = jnp.where(kind == 0, leaf, lane).astype(jnp.float32).astype(jnp.bfloat16)
        term = lax.dot_general(
            value, hit, (((1,), (1,)), ((), ())), preferred_element_type=jnp.float32
        )
        total = term if total is None else total + term
    place[...] = total.astype(jnp.int32)
    for side, out in enumerate((joint_own, joint)):
        for i in range(leaves):
            both = jnp.dot(
                mixers[mixers.shape[0] - 1, i, side], expand[i], preferred_element_type=jnp.float32
            )
            high = both.astype(jnp.bfloat16)
            out[i, :, :LANES] = high
            out[i, :, LANES:] = (both - high.astype(jnp.float32)).astype(jnp.bfloat16)


def top_send_body(places, table, received, factor, sent):
    for k in range(sent.shape[0]):
        i = read(table, places.slot(1, k))
        sent[k] = split(times(received[read(table, places.slot_piece(1, k))], factor[i]))


def top_own_body(places, table, received, factor, mixers, own):
    for i in range(own.shape[0]):
        state = split(times(received[read(table, places.piece(0, i))], factor[i]))
        own[i] = times(state, mixers[0, i, 0])


def mix_send_body(places, level, table, received, own, mixers, sent):
    for k in range(sent.shape[0]):
        i = read(table, places.slot(level + 1, k))
        piece = received[read(table, places.slot_piece(level + 1, k))]
        sent[k] = split(own[i] + times(piece, mixers[level - 1, i, 1]))


def mix_own_body(places, level, table, received, own, mixers, own_next):
    for i in range(own.shape[0]):
        other = times(received[read(table, places.piece(level, i))], mixers[level - 1, i, 1])
        own_next[i] = times(split(own[i] + other), mixers[level, i, 0])


def times_joint(pair, joint):
    both = jnp.dot(pair, joint, preferred_element_type=jnp.float32)
    rows = both.shape[0] // 2
    return (both[:rows, :LANES] + both[rows:, :LANES]) + (both[:rows, LANES:] + both[rows:, LANES:])


def base_body(
    places, level, table, received, own, mixers, joint_own, even, ordered, odd, dense, base, windows
):
    leaves, near_count = dense.shape[0], dense.shape[1]
    parity = lax.axis_index("block") & 1
    first, last = 0, leaves + REACH
    windows[pl.ds(jnp.where(parity == 0, last, first), REACH)] = even[...]
    windows[pl.ds(jnp.where(parity == 0, first, last), REACH)] = odd[...]
    windows[pl.ds(REACH, leaves)] = ordered[...]
    for i in range(leaves):
        other = times(received[read(table, places.piece(level, i))], mixers[level - 1, i, 1])
        total = times_joint(split(own[i] + other), joint_own[i])
        for n in range(near_count):
            source = windows[read(table, places.near(i, n))]
            total = total + jnp.dot(source, dense[i, n], preferred_element_type=jnp.float32)
        base[i] = total


def last_body(places, level, table, received, base, joint, place, applied, rows, sems):
    leaves = base.shape[0]
    blocks = []
    for i in range(leaves):
        piece = received[read(table, places.piece(level, i))]
        blocks.append((base[i] + times_joint(piece, joint[i])).astype(jnp.bfloat16).astype(jnp.float32))
    group = rows.shape[0] // sems.shape[0]
    copies = []
    for g in range(sems.shape[0]):
        here = slice(g * group, (g + 1) * group)
        part = [block[here] for block in blocks]
        for b in range(leaves):
            lanes = slice(b * LANES, (b + 1) * LANES)
            picked = pick_lanes(part, place[pl.ds(0, 1), lanes], place[pl.ds(1, 1), lanes])
            rows[here, lanes] = picked.astype(jnp.bfloat16)
        copies.append(pltpu.make_async_copy(rows.at[here], applied.at[here], sems.at[g]))
        copies[-1].start()
    for copy in copies:
        copy.wait()


def from_partner(x, bit):
    count = lax.axis_size("partner")
    return lax.ppermute(x, "partner", [(i, i ^ 1 << bit) for i in range(count)])


def with_neighbour(x, first):
    groups, count = lax.axis_size("partner"), lax.axis_size("block")
    to = {}
    for g in range(groups):
        for i in range(count):
            to[g * count + i] = (g ^ 1) * count + i
        for i in range(first, count - 1, 2):
            to[g * count + i], to[g * count + i + 1] = g * count + i + 1, g * count + i
    return lax.ppermute(x, ("partner", "block"), sorted(to.items()))


def on_device(
    points,
    tree_order,
    nearby_dense_blocks,
    neighbours,
    compress,
    expand,
    top_factor,
    butterfly_mixers,
    block_map,
):
    vectors, count = points.shape
    leaves, near_count = neighbours.shape
    levels = lax.axis_size("partner").bit_length() - 1
    half = leaves // 2
    places = Places(levels, leaves, near_count)
    order = tree_order.reshape(leaves, LANES)
    ints = pltpu.SMEM((leaves + 1,), jnp.int32)
    pair = jax.ShapeDtypeStruct((half, 2 * vectors, LANES), jnp.bfloat16)
    state = jax.ShapeDtypeStruct((leaves, vectors, LANES), jnp.float32)
    edge = jax.ShapeDtypeStruct((REACH, vectors, LANES), jnp.bfloat16)
    part = functools.partial
    assert levels > 2

    sent = call(
        first_body,
        pair,
        [HBM, HBM, HBM, HBM],
        [
            pltpu.VMEM(points.shape, points.dtype),
            pltpu.VMEM(order.shape, order.dtype),
            pltpu.VMEM(compress.shape, compress.dtype),
            pltpu.SMEM(block_map.shape, block_map.dtype),
            ints,
            ints,
            pltpu.SemaphoreType.DMA((4,)),
        ],
    )(points, order, compress, block_map)
    received = from_partner(sent, levels - 1)

    ordered, even, odd, table, mixers, dense, expand = call(
        part(order_body, places),
        [
            jax.ShapeDtypeStruct((leaves, vectors, LANES), jnp.bfloat16),
            edge,
            edge,
            jax.ShapeDtypeStruct((places.rows, LANES), jnp.int32),
            jax.ShapeDtypeStruct(butterfly_mixers.shape, butterfly_mixers.dtype),
            jax.ShapeDtypeStruct(nearby_dense_blocks.shape, nearby_dense_blocks.dtype),
            jax.ShapeDtypeStruct(expand.shape, expand.dtype),
        ],
        [VMEM, VMEM, HBM, HBM, HBM, HBM, HBM],
        [
            pltpu.SMEM(block_map.shape, block_map.dtype),
            pltpu.SMEM((near_count, leaves), neighbours.dtype),
            ints,
            ints,
            pltpu.SemaphoreType.DMA((5,)),
        ],
        flops=1 << 24,
    )(points, order, block_map, neighbours.T, butterfly_mixers, nearby_dense_blocks, expand)
    even = with_neighbour(even, 0)
    odd = with_neighbour(odd, 1)

    sent = call(part(top_send_body, places), pair, [VMEM] * 3)(table, received, top_factor)
    own = call(part(top_own_body, places), state, [VMEM] * 4, flops=1 << 24)(
        table, received, top_factor, mixers
    )
    wide = jax.ShapeDtypeStruct((leaves, LANES, 2 * LANES), jnp.bfloat16)
    place, joint_own, joint = call(
        prep_body,
        [jax.ShapeDtypeStruct((8, count), jnp.int32), wide, wide],
        [VMEM] * 3,
        flops=1 << 24,
    )(order, mixers, expand)

    for level in range(1, levels):
        received = from_partner(sent, levels - 1 - level)
        if level < levels - 1:
            sent = call(part(mix_send_body, places, level), pair, [VMEM] * 4)(
                table, received, own, mixers
            )
            if level < levels - 2:
                body, factors, scratch = mix_own_body, (mixers,), ()
            else:
                body = base_body
                factors = (mixers, joint_own, even, ordered, odd, dense)
                scratch = [pltpu.VMEM((leaves + 2 * REACH, vectors, LANES), jnp.bfloat16)]
            own = call(
                part(body, places, level),
                state,
                [VMEM] * (3 + len(factors)),
                scratch,
                flops=1 << 24,
            )(table, received, own, *factors)
    return call(
        part(last_body, places, levels - 1),
        jax.ShapeDtypeStruct(points.shape, points.dtype),
        [VMEM] * 5,
        [pltpu.VMEM(points.shape, points.dtype), pltpu.SemaphoreType.DMA((2,))],
        place=HBM,
    )(table, received, own, joint, place)


def solution(mesh):
    return jax.shard_map(
        on_device,
        mesh=mesh,
        in_specs=(
            P(None, ("partner", "block")),
            P(("partner", "block")),
            P(("partner", "block"), None, None, None),
            P(("partner", "block"), None),
            P(("partner", "block"), None, None),
            P(("partner", "block"), None, None),
            P(("partner", "block"), None, None),
            P(None, ("partner", "block"), None, None, None),
            P(),
        ),
        out_specs=P(None, ("partner", "block")),
        check_vma=False,
    )
```

profile of v0, /device:TPU:18, one launch (start us, length us, event | category | flops | bytes accessed | tf_op | source)
XLA Modules:
  0.0 17.9 jit_solution(10704730269402993955)
XLA Ops:
  0.0 0.0 copy-start.1
  0.0 0.0 copy-start.2
  0.0 1.3 %shard_map.92 = bf16[4,64,128]{2,1,0:T(8,128)(2,1)S(1)} custom-call(bf16[32,1024]{1,0:T(8,128)(2,1)} %points.3, s32[8,128]{1,0:T(8,128)} %bitcast.2, bf16[8,128,128]{2,1,0:T(8,128)(2,1)} %compress.1, s32[3,8]{1,0:T(4,128)} %block_map.3), custom_call_target="tpu_custom_call" | custom-call | flops 1048576 | bytes 262144 | tf_op jit(solution)/shard_map/pallas_call | solution.py:30
  1.3 1.6 %collective-permute-start = (bf16[4,64,128]{2,1,0:T(8,128)(2,1)S(1)}, bf16[4,64,128]{2,1,0:T(8,128)(2,1)S(1)}, u32[]{:S(2)}, u32[]{:S(2)}) collective-permute-start(bf16[4,64,128]{2,1,0:T(8,128)(2,1)S(1)} %shard_map.92), channel_id=1, source_target_pairs={{0,16},{4,20},{8,24},{12,28},{16,0},{20,4},{24,8},{28,12},{1,17},{... | collective-permute-start | bytes 196616 | tf_op jit(solution)/shard_map/ppermute | solution.py:271
  2.9 0.0 copy-done.1
  2.9 0.0 copy-done.2
  2.9 0.0 copy-start
  2.9 1.7 %shard_map.91 = (bf16[8,32,128]{2,1,0:T(8,128)(2,1)S(1)}, bf16[2,32,128]{2,1,0:T(8,128)(2,1)S(1)}, bf16[2,32,128]{2,1,0:T(8,128)(2,1)S(1)}, s32[72,128]{1,0:T(8,...) custom-call(bf16[32,1024]{1,0:T(8,128)(2,1)S(1)} %copy-done.1, ...), custom_call_target="tpu_custom_call" | custom-call | flops 16777216 | bytes 262144 | tf_op jit(solution)/shard_map/pallas_call | solution.py:30
  4.5 1.1 %collective-permute-done.received = bf16[4,64,128]{2,1,0:T(8,128)(2,1)S(1)} collective-permute-done((bf16[4,64,128]{2,1,0:T(8,128)(2,1)S(1)}, bf16[4,64,128]{2,1,0:T(8,128)(2,1)S(1)}, u32[]{:S(2)}, u32[]{:S(2)}) %collective-permute-start) | collective-permute-done | bytes 65568 | tf_op jit(solution)/shard_map/ppermute | solution.py:271
  5.6 0.0 copy-done
  5.6 0.2 %shard_map.93 = bf16[4,64,128]{2,1,0:T(8,128)(2,1)S(1)} custom-call(s32[72,128]{1,0:T(8,128)S(1)} %get-tuple-element.15.table, bf16[4,64,128]{2,1,0:T(8,128)(2,1)S(1)} %collective-permute-done.received, bf16[8,128,128]{2,1,0:T(8,128)(2,1)S(1)} %copy-done), custom_call_target="tpu_custom_call" | custom-call | flops 1048576 | bytes 262144 | tf_op jit(solution)/shard_map/pallas_call | solution.py:30
  5.8 0.6 %collective-permute-start.1 = (bf16[4,64,128]{2,1,0:T(8,128)(2,1)S(1)}, bf16[4,64,128]{2,1,0:T(8,128)(2,1)S(1)}, u32[]{:S(2)}, u32[]{:S(2)}) collective-permute-start(bf16[4,64,128]{2,1,0:T(8,128)(2,1)S(1)} %shard_map.93), channel_id=1, source_target_pairs={{0,8},{4,12},{8,0},{12,4},{16,24},{20,28},{24,16},{28,20},{1,9},{5... | collective-permute-start | bytes 196616 | tf_op jit(solution)/shard_map/ppermute | solution.py:271
  6.4 0.4 %shard_map.94.own = f32[8,32,128]{2,1,0:T(8,128)S(1)} custom-call(s32[72,128]{1,0:T(8,128)S(1)} %get-tuple-element.15.table, bf16[4,64,128]{2,1,0:T(8,128)(2,1)S(1)} %collective-permute-done.received, bf16[8,128,128]{2,1,0:T(8,128)(2,1)S(1)} %copy-done, bf16[2,8,2,128,128]{4,3,2,1,0:T(8,128)(2,1)S(1)} %get-tuple-element.16.mixers), custom_call_target="tpu_custom_call" | custom-call | flops 16777216 | bytes 262144 | tf_op jit(solution)/shard_map/pallas_call | solution.py:30
  6.8 3.3 %collective-permute-done.1.received = bf16[4,64,128]{2,1,0:T(8,128)(2,1)S(1)} collective-permute-done((bf16[4,64,128]{2,1,0:T(8,128)(2,1)S(1)}, bf16[4,64,128]{2,1,0:T(8,128)(2,1)S(1)}, u32[]{:S(2)}, u32[]{:S(2)}) %collective-permute-start.1) | collective-permute-done | bytes 65568 | tf_op jit(solution)/shard_map/ppermute | solution.py:271
  10.1 0.2 %shard_map.95 = bf16[4,64,128]{2,1,0:T(8,128)(2,1)S(1)} custom-call(s32[72,128]{1,0:T(8,128)S(1)} %get-tuple-element.15.table, bf16[4,64,128]{2,1,0:T(8,128)(2,1)S(1)} %collective-permute-done.1.received, f32[8,32,128]{2,1,0:T(8,128)S(1)} %shard_map.94.own, bf16[2,8,2,128,128]{4,3,2,1,0:T(8,128)(2,1)S(1)} %get-tuple-element.16.mixers), custom_call_target="tpu_custom_call" | custom-call | flops 1048576 | bytes 262144 | tf_op jit(solution)/shard_map/pallas_call | solution.py:30
  10.3 0.1 collective-permute-start.2
  10.4 1.6 %collective-permute-start.3 = (bf16[2,32,128]{2,1,0:T(8,128)(2,1)S(1)}, bf16[2,32,128]{2,1,0:T(8,128)(2,1)S(1)}, u32[]{:S(2)}, u32[]{:S(2)}) collective-permute-start(bf16[2,32,128]{2,1,0:T(8,128)(2,1)S(1)} %get-tuple-element.19), channel_id=1, source_target_pairs={{0,1},{1,0},{2,3},{3,2},{4,5},{5,4},{6,7},{7,6},{8,9},{9,8},{10,11... | collective-permute-start | bytes 49160 | tf_op jit(solution)/shard_map/ppermute | solution.py:282
  12.1 0.0 collective-permute-start.4
  12.1 0.9 %shard_map.96 = (s32[8,1024]{1,0:T(8,128)S(1)}, bf16[8,128,256]{2,1,0:T(8,128)(2,1)S(1)}, bf16[8,128,256]{2,1,0:T(8,128)(2,1)S(1)}) custom-call(s32[8,128]{1,0:T(8,128)S(1)} %bitcast.4, bf16[2,8,2,128,128]{4,3,2,1,0:T(8,128)(2,1)S(1)} %get-tuple-element.16.mixers, bf16[8,128,128]{2,1,0:T(8,128)(2,1)S(1)} %get-tuple-element.17.expand), custom_call_target="tpu_custom_call" | custom-call | flops 16777216 | bytes 262144 | tf_op jit(solution)/shard_map/pallas_call | solution.py:30
  12.9 1.3 %collective-permute-done.3.even = bf16[2,32,128]{2,1,0:T(8,128)(2,1)S(1)} collective-permute-done((bf16[2,32,128]{2,1,0:T(8,128)(2,1)S(1)}, bf16[2,32,128]{2,1,0:T(8,128)(2,1)S(1)}, u32[]{:S(2)}, u32[]{:S(2)}) %collective-permute-start.3) | collective-permute-done | bytes 16416 | tf_op jit(solution)/shard_map/ppermute | solution.py:282
  14.2 1.6 %collective-permute-done.4.odd = bf16[2,32,128]{2,1,0:T(8,128)(2,1)S(1)} collective-permute-done((bf16[2,32,128]{2,1,0:T(8,128)(2,1)S(1)}, bf16[2,32,128]{2,1,0:T(8,128)(2,1)S(1)}, u32[]{:S(2)}, u32[]{:S(2)}) %collective-permute-start.4) | collective-permute-done | bytes 16416 | tf_op jit(solution)/shard_map/ppermute | solution.py:282
  15.8 1.0 %shard_map.97.base = f32[8,32,128]{2,1,0:T(8,128)S(1)} custom-call(s32[72,128]{1,0:T(8,128)S(1)} %get-tuple-element.15.table, bf16[4,64,128]{2,1,0:T(8,128)(2,1)S(1)} %collective-permute-done.1.received, f32[8,32,128]{2,1,0:T(8,128)S(1)} %shard_map.94.own, bf16[2,8,2,128,128]{4,3,2,1,0:T(8,128)(2,1)S(1)} %get-tuple-element.16.mixers, ...), custom_call_target="tpu_custom_call" | custom-call | flops 16777216 | bytes 262144 | tf_op jit(solution)/shard_map/pallas_call | solution.py:30
  16.8 0.0 collective-permute-done.2.received
  16.8 1.2 %shard_map.98 = bf16[32,1024]{1,0:T(8,128)(2,1)} custom-call(s32[72,128]{1,0:T(8,128)S(1)} %get-tuple-element.15.table, bf16[4,64,128]{2,1,0:T(8,128)(2,1)S(1)} %collective-permute-done.2.received, f32[8,32,128]{2,1,0:T(8,128)S(1)} %shard_map.97.base, bf16[8,128,256]{2,1,0:T(8,128)(2,1)S(1)} %get-tuple-element.23.joint, s32[8,1024]{1,0:T(8,128)S(1)} %get-tuple-element.24.place), custom_call_target="tpu_custom_call" | custom-call | flops 1048576 | bytes 262144 | tf_op jit(solution)/shard_map/pallas_call | solution.py:30
Async XLA Ops:
  0.0 2.9 %copy-start.1 = (bf16[32,1024]{1,0:T(8,128)(2,1)S(1)}, bf16[32,1024]{1,0:T(8,128)(2,1)}, u32[]{:S(2)}) copy-start(bf16[32,1024]{1,0:T(8,128)(2,1)} %points.3) | copy-start | bytes 196612
  0.0 2.9 %copy-start.2 = (s32[1024]{0:T(1024)S(1)}, s32[1024]{0:T(1024)}, u32[]{:S(2)}) copy-start(s32[1024]{0:T(1024)} %param.10) | copy-start | bytes 12292
  1.3 4.3 %collective-permute-start = (bf16[4,64,128]{2,1,0:T(8,128)(2,1)S(1)}, bf16[4,64,128]{2,1,0:T(8,128)(2,1)S(1)}, u32[]{:S(2)}, u32[]{:S(2)}) collective-permute-start(bf16[4,64,128]{2,1,0:T(8,128)(2,1)S(1)} %shard_map.92), channel_id=1, source_target_pairs={{0,16},{4,20},{8,24},{12,28},{16,0},{20,4},{24,8},{28,12},{1,17},{... | collective-permute-start | bytes 196616 | tf_op jit(solution)/shard_map/ppermute | solution.py:271
  2.9 2.7 %copy-start = (bf16[8,128,128]{2,1,0:T(8,128)(2,1)S(1)}, bf16[8,128,128]{2,1,0:T(8,128)(2,1)}, u32[]{:S(2)}) copy-start(bf16[8,128,128]{2,1,0:T(8,128)(2,1)} %factor.3) | copy-start | bytes 786436
  5.8 4.3 %collective-permute-start.1 = (bf16[4,64,128]{2,1,0:T(8,128)(2,1)S(1)}, bf16[4,64,128]{2,1,0:T(8,128)(2,1)S(1)}, u32[]{:S(2)}, u32[]{:S(2)}) collective-permute-start(bf16[4,64,128]{2,1,0:T(8,128)(2,1)S(1)} %shard_map.93), channel_id=1, source_target_pairs={{0,8},{4,12},{8,0},{12,4},{16,24},{20,28},{24,16},{28,20},{1,9},{5... | collective-permute-start | bytes 196616 | tf_op jit(solution)/shard_map/ppermute | solution.py:271
  10.3 6.4 %collective-permute-start.2 = (bf16[4,64,128]{2,1,0:T(8,128)(2,1)S(1)}, bf16[4,64,128]{2,1,0:T(8,128)(2,1)S(1)}, u32[]{:S(2)}, u32[]{:S(2)}) collective-permute-start(bf16[4,64,128]{2,1,0:T(8,128)(2,1)S(1)} %shard_map.95), channel_id=1, source_target_pairs={{0,4},{4,0},{8,12},{12,8},{16,20},{20,16},{24,28},{28,24},{1,5},{5... | collective-permute-start | bytes 196616 | tf_op jit(solution)/shard_map/ppermute | solution.py:271
  10.4 3.8 %collective-permute-start.3 = (bf16[2,32,128]{2,1,0:T(8,128)(2,1)S(1)}, bf16[2,32,128]{2,1,0:T(8,128)(2,1)S(1)}, u32[]{:S(2)}, u32[]{:S(2)}) collective-permute-start(bf16[2,32,128]{2,1,0:T(8,128)(2,1)S(1)} %get-tuple-element.19), channel_id=1, source_target_pairs={{0,1},{1,0},{2,3},{3,2},{4,5},{5,4},{6,7},{7,6},{8,9},{9,8},{10,11... | collective-permute-start | bytes 49160 | tf_op jit(solution)/shard_map/ppermute | solution.py:282
  12.1 3.7 %collective-permute-start.4 = (bf16[2,32,128]{2,1,0:T(8,128)(2,1)S(1)}, bf16[2,32,128]{2,1,0:T(8,128)(2,1)S(1)}, u32[]{:S(2)}, u32[]{:S(2)}) collective-permute-start(bf16[2,32,128]{2,1,0:T(8,128)(2,1)S(1)} %get-tuple-element.21), channel_id=1, source_target_pairs={{0,4},{1,2},{2,1},{3,7},{4,0},{5,6},{6,5},{7,3},{8,12},{9,10},{10,... | collective-permute-start | bytes 49160 | tf_op jit(solution)/shard_map/ppermute | solution.py:282
where the time goes:
time: 18.1 us; the launch traced here: 17.9 us
  waiting for transfers between devices  7.25 us (40%)
  Pallas kernels  6.7 us (37%)
  starting transfers between devices  3.9 us (22%)
    pallas_call x8, Pallas kernels, bound(): run(*[pltpu.with_memory_space_constraint(a, pltpu.HBM) if s is HBM else a...  6.7 us
    ppermute x3, waiting for transfers between devices, from_partner(): return lax.ppermute(x, 'partner', [(i, i ^ 1 << bit) for i in range(count)])  4.4 us
    ppermute x2, waiting for transfers between devices, with_neighbour(): return lax.ppermute(x, ('partner', 'block'), sorted(to.items()))  2.86 us
    ppermute x3, starting transfers between devices, from_partner(): return lax.ppermute(x, 'partner', [(i, i ^ 1 << bit) for i in range(count)])  2.26 us
    ppermute x2, starting transfers between devices, with_neighbour(): return lax.ppermute(x, ('partner', 'block'), sorted(to.items()))  1.64 us
  transfers between devices with their start and end apart: 5, of which 4 were waited for; matrix products, arithmetic and copies ran while one was open for 0% of the time, Pallas kernels for 22%

commit v1 on v0

--- a/solution.py
+++ b/solution.py
@@ -99,62 +99,28 @@
     return [x[:, b * LANES : (b + 1) * LANES].astype(jnp.float32) for b in range(leaves)]
 
 
-def first_body(points, order, compress, block_map, sent, pts, idx, comp, table, slot, rank, sems):
+def first_body(
+    places, points, order, compress, block_map, near,
+    sent, table, pts, idx, comp, maps, nears, slots, ranks, sems,
+):
     leaves = idx.shape[0]
-    copies = [
-        pltpu.make_async_copy(block_map, table, sems.at[0]),
-        pltpu.make_async_copy(order, idx, sems.at[1]),
-        pltpu.make_async_copy(points, pts, sems.at[2]),
-        pltpu.make_async_copy(compress, comp, sems.at[3]),
-    ]
-    for copy in copies:
-        copy.start()
-    copies[0].wait()
-    tables(table, 0, slot, rank, leaves)
-    copies[1].wait()
-    copies[2].wait()
-    blocks = column_blocks(pts[...], leaves)
-    rows = []
-    for k in range(leaves // 2):
-        local = idx[pl.ds(slot[k], 1), :] & (leaves * LANES - 1)
-        rows.append(pick_lanes(blocks, local >> 7, local & (LANES - 1)).astype(jnp.bfloat16))
-    copies[3].wait()
-    for k in range(leaves // 2):
-        sent[k] = split(jnp.dot(rows[k], comp[slot[k]], preferred_element_type=jnp.float32))
-
-
-def order_body(
-    places, points, order, block_map, near, mixers, dense, expand,
-    ordered, even, odd, table, mixers_out, dense_out, expand_out, maps, nears, slot, rank, sems,
-):
-    leaves = order.shape[0]
     levels = maps.shape[0]
     copies = [
         pltpu.make_async_copy(block_map, maps, sems.at[0]),
         pltpu.make_async_copy(near, nears, sems.at[1]),
-        pltpu.make_async_copy(mixers, mixers_out, sems.at[2]),
-        pltpu.make_async_copy(dense, dense_out, sems.at[3]),
-        pltpu.make_async_copy(expand, expand_out, sems.at[4]),
+        pltpu.make_async_copy(order, idx, sems.at[2]),
+        pltpu.make_async_copy(points, pts, sems.at[3]),
+        pltpu.make_async_copy(compress, comp, sems.at[4]),
     ]
     for copy in copies:
         copy.start()
-    blocks = column_blocks(points[...], leaves)
-    for leaf in range(leaves):
-        local = order[pl.ds(leaf, 1), :] & (leaves * LANES - 1)
-        ordered[leaf] = pick_lanes(blocks, local >> 7, local & (LANES - 1)).astype(jnp.bfloat16)
-    block = lax.axis_index("block")
-    parity = block & 1
-    head, tail = 0, leaves - REACH
-    even[...] = ordered[pl.ds(jnp.where(parity == 0, tail, head), REACH)]
-    odd[...] = ordered[pl.ds(jnp.where(parity == 0, head, tail), REACH)]
-    base = (lax.axis_index("partner") * lax.axis_size("block") + block) * leaves
 
     def put(row, value):
         table[pl.ds(row, 1), :] = jnp.full((1, LANES), value, jnp.int32)
 
     copies[0].wait()
-    copies[1].wait()
     for level in range(levels):
+        slot, rank = slots.at[level], ranks.at[level]
         tables(maps, level, slot, rank, leaves)
         for i in range(leaves):
             put(places.piece(level, i), rank[maps[level, i]])
@@ -162,16 +128,49 @@
             for k in range(leaves // 2):
                 i = slot[k]
                 put(places.slot(level, k), i)
-                put(places.slot_piece(level, k), read(table, places.piece(level - 1, i)))
+                put(places.slot_piece(level, k), ranks[level - 1, maps[level - 1, i]])
+    copies[1].wait()
+    device = lax.axis_index("partner") * lax.axis_size("block") + lax.axis_index("block")
+    base = device * leaves
     for leaf in range(leaves):
         for n in range(nears.shape[0]):
             put(places.near(leaf, n), nears[n, leaf] - base + REACH)
-    for copy in copies[2:]:
-        copy.wait()
-
-
-def prep_body(order, mixers, expand, place, joint_own, joint):
+    copies[2].wait()
+    copies[3].wait()
+    blocks = column_blocks(pts[...], leaves)
+    rows = []
+    for k in range(leaves // 2):
+        local = idx[pl.ds(slots[0, k], 1), :] & (leaves * LANES - 1)
+        rows.append(pick_lanes(blocks, local >> 7, local & (LANES - 1)).astype(jnp.bfloat16))
+    copies[4].wait()
+    for k in range(leaves // 2):
+        product = jnp.dot(rows[k], comp[slots[0, k]], preferred_element_type=jnp.float32)
+        sent[k] = split(product)
+
+
+def order_body(points, order, ordered, even, odd):
     leaves = order.shape[0]
+    blocks = column_blocks(points[...], leaves)
+    for leaf in range(leaves):
+        local = order[pl.ds(leaf, 1), :] & (leaves * LANES - 1)
+        ordered[leaf] = pick_lanes(blocks, local >> 7, local & (LANES - 1)).astype(jnp.bfloat16)
+    parity = lax.axis_index("block") & 1
+    head, tail = 0, leaves - REACH
+    even[...] = ordered[pl.ds(jnp.where(parity == 0, tail, head), REACH)]
+    odd[...] = ordered[pl.ds(jnp.where(parity == 0, head, tail), REACH)]
+
+
+def prep_body(
+    order, mixers_in, dense_in, expand_in, place, joint_own, joint, mixers, dense, expand, sems
+):
+    leaves = order.shape[0]
+    copies = [
+        pltpu.make_async_copy(expand_in, expand, sems.at[0]),
+        pltpu.make_async_copy(mixers_in, mixers, sems.at[1]),
+        pltpu.make_async_copy(dense_in, dense, sems.at[2]),
+    ]
+    for copy in copies:
+        copy.start()
     count = leaves * LANES
     target = lax.broadcasted_iota(jnp.int32, (count, LANES), 0)
     kind = lax.broadcasted_iota(jnp.int32, (8, LANES), 0)
@@ -186,6 +185,8 @@
         )
         total = term if total is None else total + term
     place[...] = total.astype(jnp.int32)
+    copies[0].wait()
+    copies[1].wait()
     for side, out in enumerate((joint_own, joint)):
         for i in range(leaves):
             both = jnp.dot(
@@ -194,6 +195,7 @@
             high = both.astype(jnp.bfloat16)
             out[i, :, :LANES] = high
             out[i, :, LANES:] = (both - high.astype(jnp.float32)).astype(jnp.bfloat16)
+    copies[2].wait()
 
 
 def top_send_body(places, table, received, factor, sent):
@@ -299,64 +301,57 @@
     half = leaves // 2
     places = Places(levels, leaves, near_count)
     order = tree_order.reshape(leaves, LANES)
-    ints = pltpu.SMEM((leaves + 1,), jnp.int32)
+    ints = pltpu.SMEM((levels, leaves + 1), jnp.int32)
     pair = jax.ShapeDtypeStruct((half, 2 * vectors, LANES), jnp.bfloat16)
     state = jax.ShapeDtypeStruct((leaves, vectors, LANES), jnp.float32)
     edge = jax.ShapeDtypeStruct((REACH, vectors, LANES), jnp.bfloat16)
     part = functools.partial
     assert levels > 2
 
-    sent = call(
-        first_body,
-        pair,
-        [HBM, HBM, HBM, HBM],
+    sent, table = call(
+        part(first_body, places),
+        [pair, jax.ShapeDtypeStruct((places.rows, LANES), jnp.int32)],
+        [HBM] * 5,
         [
             pltpu.VMEM(points.shape, points.dtype),
             pltpu.VMEM(order.shape, order.dtype),
             pltpu.VMEM(compress.shape, compress.dtype),
-            pltpu.SMEM(block_map.shape, block_map.dtype),
-            ints,
-            ints,
-            pltpu.SemaphoreType.DMA((4,)),
-        ],
-    )(points, order, compress, block_map)
-    received = from_partner(sent, levels - 1)
-
-    ordered, even, odd, table, mixers, dense, expand = call(
-        part(order_body, places),
-        [
-            jax.ShapeDtypeStruct((leaves, vectors, LANES), jnp.bfloat16),
-            edge,
-            edge,
-            jax.ShapeDtypeStruct((places.rows, LANES), jnp.int32),
-            jax.ShapeDtypeStruct(butterfly_mixers.shape, butterfly_mixers.dtype),
-            jax.ShapeDtypeStruct(nearby_dense_blocks.shape, nearby_dense_blocks.dtype),
-            jax.ShapeDtypeStruct(expand.shape, expand.dtype),
-        ],
-        [VMEM, VMEM, HBM, HBM, HBM, HBM, HBM],
-        [
             pltpu.SMEM(block_map.shape, block_map.dtype),
             pltpu.SMEM((near_count, leaves), neighbours.dtype),
             ints,
             ints,
             pltpu.SemaphoreType.DMA((5,)),
         ],
+    )(points, order, compress, block_map, neighbours.T)
+    received = from_partner(sent, levels - 1)
+
+    ordered, even, odd = call(
+        order_body,
+        [jax.ShapeDtypeStruct((leaves, vectors, LANES), jnp.bfloat16), edge, edge],
+        [VMEM] * 2,
         flops=1 << 24,
-    )(points, order, block_map, neighbours.T, butterfly_mixers, nearby_dense_blocks, expand)
+    )(points, order)
     even = with_neighbour(even, 0)
     odd = with_neighbour(odd, 1)
 
     sent = call(part(top_send_body, places), pair, [VMEM] * 3)(table, received, top_factor)
+    wide = jax.ShapeDtypeStruct((leaves, LANES, 2 * LANES), jnp.bfloat16)
+    place, joint_own, joint, mixers, dense = call(
+        prep_body,
+        [
+            jax.ShapeDtypeStruct((8, count), jnp.int32),
+            wide,
+            wide,
+            jax.ShapeDtypeStruct(butterfly_mixers.shape, butterfly_mixers.dtype),
+            jax.ShapeDtypeStruct(nearby_dense_blocks.shape, nearby_dense_blocks.dtype),
+        ],
+        [VMEM] + [HBM] * 3,
+        [pltpu.VMEM(expand.shape, expand.dtype), pltpu.SemaphoreType.DMA((3,))],
+        flops=1 << 24,
+    )(order, butterfly_mixers, nearby_dense_blocks, expand)
     own = call(part(top_own_body, places), state, [VMEM] * 4, flops=1 << 24)(
         table, received, top_factor, mixers
     )
-    wide = jax.ShapeDtypeStruct((leaves, LANES, 2 * LANES), jnp.bfloat16)
-    place, joint_own, joint = call(
-        prep_body,
-        [jax.ShapeDtypeStruct((8, count), jnp.int32), wide, wide],
-        [VMEM] * 3,
-        flops=1 << 24,
-    )(order, mixers, expand)
 
     for level in range(1, levels):
         received = from_partner(sent, levels - 1 - level)

time: 18.1 us -> 18.8 us (1.039)
  the two profiles are of different devices: /device:TPU:18 before, /device:TPU:0 now
where the time goes in v1:
time: 18.8 us; the launch traced here: 18.5 us
  starting transfers between devices  6.83 us (36%)
  Pallas kernels  6.6 us (35%)
  waiting for transfers between devices  4.41 us (23%)
  local copies, waits for them, and re-layouts  0.56 us (3%)
    pallas_call x8, Pallas kernels, bound(): run(*[pltpu.with_memory_space_constraint(a, pltpu.HBM) if s is HBM else a...  6.6 us
    ppermute x3, starting transfers between devices, from_partner(): return lax.ppermute(x, 'partner', [(i, i ^ 1 << bit) for i in range(count)])  5.19 us
    ppermute x3, waiting for transfers between devices, from_partner(): return lax.ppermute(x, 'partner', [(i, i ^ 1 << bit) for i in range(count)])  2.25 us
    ppermute x2, waiting for transfers between devices, with_neighbour(): return lax.ppermute(x, ('partner', 'block'), sorted(to.items()))  2.16 us
    ppermute x2, starting transfers between devices, with_neighbour(): return lax.ppermute(x, ('partner', 'block'), sorted(to.items()))  1.64 us
    unnamed x6, local copies, waits for them, and re-layouts  0.56 us
  transfers between devices with their start and end apart: 5, of which 2 were waited for; matrix products, arithmetic and copies ran while one was open for 0% of the time, Pallas kernels for 20%

profile of v1, /device:TPU:0, one launch (start us, length us, event | category | flops | bytes accessed | tf_op | source)
XLA Modules:
  0.0 18.5 jit_solution(5911181502210296114)
XLA Ops:
  0.0 0.0 copy-start
  0.0 1.3 %shard_map.91 = (bf16[4,64,128]{2,1,0:T(8,128)(2,1)S(1)}, s32[72,128]{1,0:T(8,128)S(1)}) custom-call(bf16[32,1024]{1,0:T(8,128)(2,1)} %points.3, s32[8,128]{1,0:T(8,128)} %bitcast.2, bf16[8,128,128]{2,1,0:T(8,128)(2,1)} %compress.1, s32[3,8]{1,0:T(4,128)} %block_map.1, s32[3,8]{1,0:T(4,128)} %bitcast.5), custom_call_target="tpu_custom_call" | custom-call | flops 1048576 | bytes 262144 | tf_op jit(solution)/shard_map/pallas_call | solution.py:30
  1.3 3.1 %collective-permute-start = (bf16[4,64,128]{2,1,0:T(8,128)(2,1)S(1)}, bf16[4,64,128]{2,1,0:T(8,128)(2,1)S(1)}, u32[]{:S(2)}, u32[]{:S(2)}) collective-permute-start(bf16[4,64,128]{2,1,0:T(8,128)(2,1)S(1)} %get-tuple-element.16), channel_id=1, source_target_pairs={{0,16},{4,20},{8,24},{12,28},{16,0},{20,4},{24,8},{28,12},{1,17},{... | collective-permute-start | bytes 196616 | tf_op jit(solution)/shard_map/ppermute | solution.py:273
  4.4 2.2 %collective-permute-done.received = bf16[4,64,128]{2,1,0:T(8,128)(2,1)S(1)} collective-permute-done((bf16[4,64,128]{2,1,0:T(8,128)(2,1)S(1)}, bf16[4,64,128]{2,1,0:T(8,128)(2,1)S(1)}, u32[]{:S(2)}, u32[]{:S(2)}) %collective-permute-start) | collective-permute-done | bytes 65568 | tf_op jit(solution)/shard_map/ppermute | solution.py:273
  6.6 0.0 copy-done
  6.6 0.0 copy-start.2
  6.6 0.2 %shard_map.92 = bf16[4,64,128]{2,1,0:T(8,128)(2,1)S(1)} custom-call(s32[72,128]{1,0:T(8,128)S(1)} %get-tuple-element.15.table, bf16[4,64,128]{2,1,0:T(8,128)(2,1)S(1)} %collective-permute-done.received, bf16[8,128,128]{2,1,0:T(8,128)(2,1)S(1)} %copy-done), custom_call_target="tpu_custom_call" | custom-call | flops 1048576 | bytes 262144 | tf_op jit(solution)/shard_map/pallas_call | solution.py:30
  6.8 2.1 %collective-permute-start.1 = (bf16[4,64,128]{2,1,0:T(8,128)(2,1)S(1)}, bf16[4,64,128]{2,1,0:T(8,128)(2,1)S(1)}, u32[]{:S(2)}, u32[]{:S(2)}) collective-permute-start(bf16[4,64,128]{2,1,0:T(8,128)(2,1)S(1)} %shard_map.92), channel_id=1, source_target_pairs={{0,8},{4,12},{8,0},{12,4},{16,24},{20,28},{24,16},{28,20},{1,9},{5... | collective-permute-start | bytes 196616 | tf_op jit(solution)/shard_map/ppermute | solution.py:273
  8.9 0.0 copy-done.2
  8.9 2.1 %shard_map.93 = (s32[8,1024]{1,0:T(8,128)S(1)}, bf16[8,128,256]{2,1,0:T(8,128)(2,1)S(1)}, bf16[8,128,256]{2,1,0:T(8,128)(2,1)S(1)}, bf16[2,8,2,128,128]{4,3,2,1,0:T(8,128)(2,1)S(1)}, bf16[8,3,128,128]{3,2,1,0:T(8,128)(2,1)S(1)}) custom-call(s32[8,128]{1,0:T(8,128)S(1)} %bitcast.3, bf16[2,8,2,128,128]{4,3,2,1,0:T(8,128)(2,1)} %mixers_in.1, ...), custom_call_target="tpu_custom_call" | custom-call | flops 16777216 | bytes 262144 | tf_op jit(solution)/shard_map/pallas_call | solution.py:30
  11.0 0.4 %shard_map.94.own = f32[8,32,128]{2,1,0:T(8,128)S(1)} custom-call(s32[72,128]{1,0:T(8,128)S(1)} %get-tuple-element.15.table, bf16[4,64,128]{2,1,0:T(8,128)(2,1)S(1)} %collective-permute-done.received, bf16[8,128,128]{2,1,0:T(8,128)(2,1)S(1)} %copy-done, bf16[2,8,2,128,128]{4,3,2,1,0:T(8,128)(2,1)S(1)} %get-tuple-element.17.mixers), custom_call_target="tpu_custom_call" | custom-call | flops 16777216 | bytes 262144 | tf_op jit(solution)/shard_map/pallas_call | solution.py:30
  11.4 0.0 copy-start.1
  11.4 0.0 collective-permute-done.1.received
  11.4 0.2 %shard_map.95 = bf16[4,64,128]{2,1,0:T(8,128)(2,1)S(1)} custom-call(s32[72,128]{1,0:T(8,128)S(1)} %get-tuple-element.15.table, bf16[4,64,128]{2,1,0:T(8,128)(2,1)S(1)} %collective-permute-done.1.received, f32[8,32,128]{2,1,0:T(8,128)S(1)} %shard_map.94.own, bf16[2,8,2,128,128]{4,3,2,1,0:T(8,128)(2,1)S(1)} %get-tuple-element.17.mixers), custom_call_target="tpu_custom_call" | custom-call | flops 1048576 | bytes 262144 | tf_op jit(solution)/shard_map/pallas_call | solution.py:30
  11.6 0.1 collective-permute-start.2
  11.7 0.6 %copy-done.1 = bf16[32,1024]{1,0:T(8,128)(2,1)S(1)} copy-done((bf16[32,1024]{1,0:T(8,128)(2,1)S(1)}, bf16[32,1024]{1,0:T(8,128)(2,1)}, u32[]{:S(2)}) %copy-start.1) | copy-done | bytes 65560
  12.3 0.2 %shard_map.96 = (bf16[8,32,128]{2,1,0:T(8,128)(2,1)S(1)}, bf16[2,32,128]{2,1,0:T(8,128)(2,1)S(1)}, bf16[2,32,128]{2,1,0:T(8,128)(2,1)S(1)}) custom-call(bf16[32,1024]{1,0:T(8,128)(2,1)S(1)} %copy-done.1, s32[8,128]{1,0:T(8,128)S(1)} %bitcast.4), custom_call_target="tpu_custom_call" | custom-call | flops 16777216 | bytes 262144 | tf_op jit(solution)/shard_map/pallas_call | solution.py:30
  12.5 1.6 %collective-permute-start.3 = (bf16[2,32,128]{2,1,0:T(8,128)(2,1)S(1)}, bf16[2,32,128]{2,1,0:T(8,128)(2,1)S(1)}, u32[]{:S(2)}, u32[]{:S(2)}) collective-permute-start(bf16[2,32,128]{2,1,0:T(8,128)(2,1)S(1)} %get-tuple-element.19), channel_id=1, source_target_pairs={{0,1},{1,0},{2,3},{3,2},{4,5},{5,4},{6,7},{7,6},{8,9},{9,8},{10,11... | collective-permute-start | bytes 49160 | tf_op jit(solution)/shard_map/ppermute | solution.py:284
  14.2 0.0 collective-permute-start.4
  14.2 2.2 %collective-permute-done.3.even = bf16[2,32,128]{2,1,0:T(8,128)(2,1)S(1)} collective-permute-done((bf16[2,32,128]{2,1,0:T(8,128)(2,1)S(1)}, bf16[2,32,128]{2,1,0:T(8,128)(2,1)S(1)}, u32[]{:S(2)}, u32[]{:S(2)}) %collective-permute-start.3) | collective-permute-done | bytes 16416 | tf_op jit(solution)/shard_map/ppermute | solution.py:284
  16.3 0.0 collective-permute-done.4.odd
  16.3 1.0 %shard_map.97.base = f32[8,32,128]{2,1,0:T(8,128)S(1)} custom-call(s32[72,128]{1,0:T(8,128)S(1)} %get-tuple-element.15.table, bf16[4,64,128]{2,1,0:T(8,128)(2,1)S(1)} %collective-permute-done.1.received, f32[8,32,128]{2,1,0:T(8,128)S(1)} %shard_map.94.own, bf16[2,8,2,128,128]{4,3,2,1,0:T(8,128)(2,1)S(1)} %get-tuple-element.17.mixers, ...), custom_call_target="tpu_custom_call" | custom-call | flops 16777216 | bytes 262144 | tf_op jit(solution)/shard_map/pallas_call | solution.py:30
  17.3 0.0 collective-permute-done.2.received
  17.3 1.2 %shard_map.98 = bf16[32,1024]{1,0:T(8,128)(2,1)} custom-call(s32[72,128]{1,0:T(8,128)S(1)} %get-tuple-element.15.table, bf16[4,64,128]{2,1,0:T(8,128)(2,1)S(1)} %collective-permute-done.2.received, f32[8,32,128]{2,1,0:T(8,128)S(1)} %shard_map.97.base, bf16[8,128,256]{2,1,0:T(8,128)(2,1)S(1)} %get-tuple-element.23.joint, s32[8,1024]{1,0:T(8,128)S(1)} %get-tuple-element.24.place), custom_call_target="tpu_custom_call" | custom-call | flops 1048576 | bytes 262144 | tf_op jit(solution)/shard_map/pallas_call | solution.py:30
Async XLA Ops:
  0.0 6.6 %copy-start = (bf16[8,128,128]{2,1,0:T(8,128)(2,1)S(1)}, bf16[8,128,128]{2,1,0:T(8,128)(2,1)}, u32[]{:S(2)}) copy-start(bf16[8,128,128]{2,1,0:T(8,128)(2,1)} %factor.3) | copy-start | bytes 786436
  1.3 5.3 %collective-permute-start = (bf16[4,64,128]{2,1,0:T(8,128)(2,1)S(1)}, bf16[4,64,128]{2,1,0:T(8,128)(2,1)S(1)}, u32[]{:S(2)}, u32[]{:S(2)}) collective-permute-start(bf16[4,64,128]{2,1,0:T(8,128)(2,1)S(1)} %get-tuple-element.16), channel_id=1, source_target_pairs={{0,16},{4,20},{8,24},{12,28},{16,0},{20,4},{24,8},{28,12},{1,17},{... | collective-permute-start | bytes 196616 | tf_op jit(solution)/shard_map/ppermute | solution.py:273
  6.6 2.3 %copy-start.2 = (s32[1024]{0:T(1024)S(1)}, s32[1024]{0:T(1024)}, u32[]{:S(2)}) copy-start(s32[1024]{0:T(1024)} %param.10) | copy-start | bytes 12292
  6.8 4.6 %collective-permute-start.1 = (bf16[4,64,128]{2,1,0:T(8,128)(2,1)S(1)}, bf16[4,64,128]{2,1,0:T(8,128)(2,1)S(1)}, u32[]{:S(2)}, u32[]{:S(2)}) collective-permute-start(bf16[4,64,128]{2,1,0:T(8,128)(2,1)S(1)} %shard_map.92), channel_id=1, source_target_pairs={{0,8},{4,12},{8,0},{12,4},{16,24},{20,28},{24,16},{28,20},{1,9},{5... | collective-permute-start | bytes 196616 | tf_op jit(solution)/shard_map/ppermute | solution.py:273
  11.4 0.9 %copy-start.1 = (bf16[32,1024]{1,0:T(8,128)(2,1)S(1)}, bf16[32,1024]{1,0:T(8,128)(2,1)}, u32[]{:S(2)}) copy-start(bf16[32,1024]{1,0:T(8,128)(2,1)} %points.3) | copy-start | bytes 196612
  11.6 5.6 %collective-permute-start.2 = (bf16[4,64,128]{2,1,0:T(8,128)(2,1)S(1)}, bf16[4,64,128]{2,1,0:T(8,128)(2,1)S(1)}, u32[]{:S(2)}, u32[]{:S(2)}) collective-permute-start(bf16[4,64,128]{2,1,0:T(8,128)(2,1)S(1)} %shard_map.95), channel_id=1, source_target_pairs={{0,4},{4,0},{8,12},{12,8},{16,20},{20,16},{24,28},{28,24},{1,5},{5... | collective-permute-start | bytes 196616 | tf_op jit(solution)/shard_map/ppermute | solution.py:273
  12.5 3.8 %collective-permute-start.3 = (bf16[2,32,128]{2,1,0:T(8,128)(2,1)S(1)}, bf16[2,32,128]{2,1,0:T(8,128)(2,1)S(1)}, u32[]{:S(2)}, u32[]{:S(2)}) collective-permute-start(bf16[2,32,128]{2,1,0:T(8,128)(2,1)S(1)} %get-tuple-element.19), channel_id=1, source_target_pairs={{0,1},{1,0},{2,3},{3,2},{4,5},{5,4},{6,7},{7,6},{8,9},{9,8},{10,11... | collective-permute-start | bytes 49160 | tf_op jit(solution)/shard_map/ppermute | solution.py:284
  14.2 2.2 %collective-permute-start.4 = (bf16[2,32,128]{2,1,0:T(8,128)(2,1)S(1)}, bf16[2,32,128]{2,1,0:T(8,128)(2,1)S(1)}, u32[]{:S(2)}, u32[]{:S(2)}) collective-permute-start(bf16[2,32,128]{2,1,0:T(8,128)(2,1)S(1)} %get-tuple-element.21), channel_id=1, source_target_pairs={{0,4},{1,2},{2,1},{3,7},{4,0},{5,6},{6,5},{7,3},{8,12},{9,10},{10,... | collective-permute-start | bytes 49160 | tf_op jit(solution)/shard_map/ppermute | solution.py:284

commit v2 on v1

--- a/solution.py
+++ b/solution.py
@@ -161,16 +161,11 @@
 
 
 def prep_body(
-    order, mixers_in, dense_in, expand_in, place, joint_own, joint, mixers, dense, expand, sems
+    order, expand, mixers_in, place, joint_own, joint, mixers, sem
 ):
     leaves = order.shape[0]
-    copies = [
-        pltpu.make_async_copy(expand_in, expand, sems.at[0]),
-        pltpu.make_async_copy(mixers_in, mixers, sems.at[1]),
-        pltpu.make_async_copy(dense_in, dense, sems.at[2]),
-    ]
-    for copy in copies:
-        copy.start()
+    copy = pltpu.make_async_copy(mixers_in, mixers, sem)
+    copy.start()
     count = leaves * LANES
     target = lax.broadcasted_iota(jnp.int32, (count, LANES), 0)
     kind = lax.broadcasted_iota(jnp.int32, (8, LANES), 0)
@@ -185,8 +180,7 @@
         )
         total = term if total is None else total + term
     place[...] = total.astype(jnp.int32)
-    copies[0].wait()
-    copies[1].wait()
+    copy.wait()
     for side, out in enumerate((joint_own, joint)):
         for i in range(leaves):
             both = jnp.dot(
@@ -195,7 +189,6 @@
             high = both.astype(jnp.bfloat16)
             out[i, :, :LANES] = high
             out[i, :, LANES:] = (both - high.astype(jnp.float32)).astype(jnp.bfloat16)
-    copies[2].wait()
 
 
 def top_send_body(places, table, received, factor, sent):
@@ -336,19 +329,18 @@
 
     sent = call(part(top_send_body, places), pair, [VMEM] * 3)(table, received, top_factor)
     wide = jax.ShapeDtypeStruct((leaves, LANES, 2 * LANES), jnp.bfloat16)
-    place, joint_own, joint, mixers, dense = call(
+    place, joint_own, joint, mixers = call(
         prep_body,
         [
             jax.ShapeDtypeStruct((8, count), jnp.int32),
             wide,
             wide,
             jax.ShapeDtypeStruct(butterfly_mixers.shape, butterfly_mixers.dtype),
-            jax.ShapeDtypeStruct(nearby_dense_blocks.shape, nearby_dense_blocks.dtype),
         ],
-        [VMEM] + [HBM] * 3,
-        [pltpu.VMEM(expand.shape, expand.dtype), pltpu.SemaphoreType.DMA((3,))],
+        [VMEM, VMEM, HBM],
+        [pltpu.SemaphoreType.DMA],
         flops=1 << 24,
-    )(order, butterfly_mixers, nearby_dense_blocks, expand)
+    )(order, expand, butterfly_mixers)
     own = call(part(top_own_body, places), state, [VMEM] * 4, flops=1 << 24)(
         table, received, top_factor, mixers
     )
@@ -363,7 +355,7 @@
                 body, factors, scratch = mix_own_body, (mixers,), ()
             else:
                 body = base_body
-                factors = (mixers, joint_own, even, ordered, odd, dense)
+                factors = (mixers, joint_own, even, ordered, odd, nearby_dense_blocks)
                 scratch = [pltpu.VMEM((leaves + 2 * REACH, vectors, LANES), jnp.bfloat16)]
             own = call(
                 part(body, places, level),

time: 18.8 us -> 18.4 us (0.979)
  the two profiles are of different devices: /device:TPU:0 before, /device:TPU:18 now
where the time goes in v2:
time: 18.4 us; the launch traced here: 18.3 us
  waiting for transfers between devices  8.23 us (45%)
  Pallas kernels  6.03 us (33%)
  starting transfers between devices  3.9 us (21%)
    pallas_call x8, Pallas kernels, bound(): run(*[pltpu.with_memory_space_constraint(a, pltpu.HBM) if s is HBM else a...  6.03 us
    ppermute x3, waiting for transfers between devices, from_partner(): return lax.ppermute(x, 'partner', [(i, i ^ 1 << bit) for i in range(count)])  4.49 us
    ppermute x2, waiting for transfers between devices, with_neighbour(): return lax.ppermute(x, ('partner', 'block'), sorted(to.items()))  3.74 us
    ppermute x3, starting transfers between devices, from_partner(): return lax.ppermute(x, 'partner', [(i, i ^ 1 << bit) for i in range(count)])  2.26 us
    ppermute x2, starting transfers between devices, with_neighbour(): return lax.ppermute(x, ('partner', 'block'), sorted(to.items()))  1.64 us
  transfers between devices with their start and end apart: 5, of which 4 were waited for; matrix products, arithmetic and copies ran while one was open for 0% of the time, Pallas kernels for 17%

profile of v2, /device:TPU:18, one launch (start us, length us, event | category | flops | bytes accessed | tf_op | source)
XLA Modules:
  0.0 18.3 jit_solution(8594136136343959238)
XLA Ops:
  0.0 0.0 copy-start
  0.0 1.3 %shard_map.91 = (bf16[4,64,128]{2,1,0:T(8,128)(2,1)S(1)}, s32[72,128]{1,0:T(8,128)S(1)}) custom-call(bf16[32,1024]{1,0:T(8,128)(2,1)} %points.3, s32[8,128]{1,0:T(8,128)} %bitcast.2, bf16[8,128,128]{2,1,0:T(8,128)(2,1)} %compress.1, s32[3,8]{1,0:T(4,128)} %block_map.1, s32[3,8]{1,0:T(4,128)} %bitcast.5), custom_call_target="tpu_custom_call" | custom-call | flops 1048576 | bytes 262144 | tf_op jit(solution)/shard_map/pallas_call | solution.py:30
  1.3 0.0 copy-start.2
  1.3 1.6 %collective-permute-start = (bf16[4,64,128]{2,1,0:T(8,128)(2,1)S(1)}, bf16[4,64,128]{2,1,0:T(8,128)(2,1)S(1)}, u32[]{:S(2)}, u32[]{:S(2)}) collective-permute-start(bf16[4,64,128]{2,1,0:T(8,128)(2,1)S(1)} %get-tuple-element.15), channel_id=1, source_target_pairs={{0,16},{4,20},{8,24},{12,28},{16,0},{20,4},{24,8},{28,12},{1,17},{... | collective-permute-start | bytes 196616 | tf_op jit(solution)/shard_map/ppermute | solution.py:266
  2.9 2.7 %collective-permute-done.received = bf16[4,64,128]{2,1,0:T(8,128)(2,1)S(1)} collective-permute-done((bf16[4,64,128]{2,1,0:T(8,128)(2,1)S(1)}, bf16[4,64,128]{2,1,0:T(8,128)(2,1)S(1)}, u32[]{:S(2)}, u32[]{:S(2)}) %collective-permute-start) | collective-permute-done | bytes 65568 | tf_op jit(solution)/shard_map/ppermute | solution.py:266
  5.7 0.0 copy-done
  5.7 0.0 copy-start.4
  5.7 0.2 %shard_map.92 = bf16[4,64,128]{2,1,0:T(8,128)(2,1)S(1)} custom-call(s32[72,128]{1,0:T(8,128)S(1)} %get-tuple-element.14.table, bf16[4,64,128]{2,1,0:T(8,128)(2,1)S(1)} %collective-permute-done.received, bf16[8,128,128]{2,1,0:T(8,128)(2,1)S(1)} %copy-done), custom_call_target="tpu_custom_call" | custom-call | flops 1048576 | bytes 262144 | tf_op jit(solution)/shard_map/pallas_call | solution.py:30
  5.9 0.6 %collective-permute-start.1 = (bf16[4,64,128]{2,1,0:T(8,128)(2,1)S(1)}, bf16[4,64,128]{2,1,0:T(8,128)(2,1)S(1)}, u32[]{:S(2)}, u32[]{:S(2)}) collective-permute-start(bf16[4,64,128]{2,1,0:T(8,128)(2,1)S(1)} %shard_map.92), channel_id=1, source_target_pairs={{0,8},{4,12},{8,0},{12,4},{16,24},{20,28},{24,16},{28,20},{1,9},{5... | collective-permute-start | bytes 196616 | tf_op jit(solution)/shard_map/ppermute | solution.py:266
  6.5 0.0 copy-done.2
  6.5 0.0 copy-done.4
  6.5 1.6 %shard_map.93 = (s32[8,1024]{1,0:T(8,128)S(1)}, bf16[8,128,256]{2,1,0:T(8,128)(2,1)S(1)}, bf16[8,128,256]{2,1,0:T(8,128)(2,1)S(1)}, bf16[2,8,2,128,128]{4,3,2,1,0:T(8,128)(2,1)S(1)}) custom-call(s32[8,128]{1,0:T(8,128)S(1)} %bitcast.3, bf16[8,128,128]{2,1,0:T(8,128)(2,1)S(1)} %copy-done.2, bf16[2,8,2,128,128]{4,3,2,1,0:T(8,128)(2,1)} %mixers_in.1), custom_call_target="tpu_custom_call" | custom-call | flops 16777216 | bytes 262144 | tf_op jit(solution)/shard_map/pallas_call | solution.py:30
  8.0 0.4 %shard_map.94.own = f32[8,32,128]{2,1,0:T(8,128)S(1)} custom-call(s32[72,128]{1,0:T(8,128)S(1)} %get-tuple-element.14.table, bf16[4,64,128]{2,1,0:T(8,128)(2,1)S(1)} %collective-permute-done.received, bf16[8,128,128]{2,1,0:T(8,128)(2,1)S(1)} %copy-done, bf16[2,8,2,128,128]{4,3,2,1,0:T(8,128)(2,1)S(1)} %get-tuple-element.16.mixers), custom_call_target="tpu_custom_call" | custom-call | flops 16777216 | bytes 262144 | tf_op jit(solution)/shard_map/pallas_call | solution.py:30
  8.4 0.0 copy-start.3
  8.4 0.0 copy-start.1
  8.5 1.7 %collective-permute-done.1.received = bf16[4,64,128]{2,1,0:T(8,128)(2,1)S(1)} collective-permute-done((bf16[4,64,128]{2,1,0:T(8,128)(2,1)S(1)}, bf16[4,64,128]{2,1,0:T(8,128)(2,1)S(1)}, u32[]{:S(2)}, u32[]{:S(2)}) %collective-permute-start.1) | collective-permute-done | bytes 65568 | tf_op jit(solution)/shard_map/ppermute | solution.py:266
  10.2 0.2 %shard_map.95 = bf16[4,64,128]{2,1,0:T(8,128)(2,1)S(1)} custom-call(s32[72,128]{1,0:T(8,128)S(1)} %get-tuple-element.14.table, bf16[4,64,128]{2,1,0:T(8,128)(2,1)S(1)} %collective-permute-done.1.received, f32[8,32,128]{2,1,0:T(8,128)S(1)} %shard_map.94.own, bf16[2,8,2,128,128]{4,3,2,1,0:T(8,128)(2,1)S(1)} %get-tuple-element.16.mixers), custom_call_target="tpu_custom_call" | custom-call | flops 1048576 | bytes 262144 | tf_op jit(solution)/shard_map/pallas_call | solution.py:30
  10.4 0.1 collective-permute-start.2
  10.5 0.0 copy-done.3
  10.5 0.2 %shard_map.96 = (bf16[8,32,128]{2,1,0:T(8,128)(2,1)S(1)}, bf16[2,32,128]{2,1,0:T(8,128)(2,1)S(1)}, bf16[2,32,128]{2,1,0:T(8,128)(2,1)S(1)}) custom-call(bf16[32,1024]{1,0:T(8,128)(2,1)S(1)} %copy-done.3, s32[8,128]{1,0:T(8,128)S(1)} %bitcast.4), custom_call_target="tpu_custom_call" | custom-call | flops 16777216 | bytes 262144 | tf_op jit(solution)/shard_map/pallas_call | solution.py:30
  10.7 1.6 %collective-permute-start.3 = (bf16[2,32,128]{2,1,0:T(8,128)(2,1)S(1)}, bf16[2,32,128]{2,1,0:T(8,128)(2,1)S(1)}, u32[]{:S(2)}, u32[]{:S(2)}) collective-permute-start(bf16[2,32,128]{2,1,0:T(8,128)(2,1)S(1)} %get-tuple-element.18), channel_id=1, source_target_pairs={{0,1},{1,0},{2,3},{3,2},{4,5},{5,4},{6,7},{7,6},{8,9},{9,8},{10,11... | collective-permute-start | bytes 49160 | tf_op jit(solution)/shard_map/ppermute | solution.py:277
  12.4 0.0 collective-permute-start.4
  12.4 2.2 %collective-permute-done.3.even = bf16[2,32,128]{2,1,0:T(8,128)(2,1)S(1)} collective-permute-done((bf16[2,32,128]{2,1,0:T(8,128)(2,1)S(1)}, bf16[2,32,128]{2,1,0:T(8,128)(2,1)S(1)}, u32[]{:S(2)}, u32[]{:S(2)}) %collective-permute-start.3) | collective-permute-done | bytes 16416 | tf_op jit(solution)/shard_map/ppermute | solution.py:277
  14.5 1.6 %collective-permute-done.4.odd = bf16[2,32,128]{2,1,0:T(8,128)(2,1)S(1)} collective-permute-done((bf16[2,32,128]{2,1,0:T(8,128)(2,1)S(1)}, bf16[2,32,128]{2,1,0:T(8,128)(2,1)S(1)}, u32[]{:S(2)}, u32[]{:S(2)}) %collective-permute-start.4) | collective-permute-done | bytes 16416 | tf_op jit(solution)/shard_map/ppermute | solution.py:277
  16.1 0.0 copy-done.1
  16.1 1.0 %shard_map.97.base = f32[8,32,128]{2,1,0:T(8,128)S(1)} custom-call(s32[72,128]{1,0:T(8,128)S(1)} %get-tuple-element.14.table, bf16[4,64,128]{2,1,0:T(8,128)(2,1)S(1)} %collective-permute-done.1.received, f32[8,32,128]{2,1,0:T(8,128)S(1)} %shard_map.94.own, bf16[2,8,2,128,128]{4,3,2,1,0:T(8,128)(2,1)S(1)} %get-tuple-element.16.mixers, ...), custom_call_target="tpu_custom_call" | custom-call | flops 16777216 | bytes 262144 | tf_op jit(solution)/shard_map/pallas_call | solution.py:30
  17.1 0.0 collective-permute-done.2.received
  17.1 1.2 %shard_map.98 = bf16[32,1024]{1,0:T(8,128)(2,1)} custom-call(s32[72,128]{1,0:T(8,128)S(1)} %get-tuple-element.14.table, bf16[4,64,128]{2,1,0:T(8,128)(2,1)S(1)} %collective-permute-done.2.received, f32[8,32,128]{2,1,0:T(8,128)S(1)} %shard_map.97.base, bf16[8,128,256]{2,1,0:T(8,128)(2,1)S(1)} %get-tuple-element.21.joint, s32[8,1024]{1,0:T(8,128)S(1)} %get-tuple-element.22.place), custom_call_target="tpu_custom_call" | custom-call | flops 1048576 | bytes 262144 | tf_op jit(solution)/shard_map/pallas_call | solution.py:30
Async XLA Ops:
  0.0 5.7 %copy-start = (bf16[8,128,128]{2,1,0:T(8,128)(2,1)S(1)}, bf16[8,128,128]{2,1,0:T(8,128)(2,1)}, u32[]{:S(2)}) copy-start(bf16[8,128,128]{2,1,0:T(8,128)(2,1)} %factor.3) | copy-start | bytes 786436
  1.3 5.1 %copy-start.2 = (bf16[8,128,128]{2,1,0:T(8,128)(2,1)S(1)}, bf16[8,128,128]{2,1,0:T(8,128)(2,1)}, u32[]{:S(2)}) copy-start(bf16[8,128,128]{2,1,0:T(8,128)(2,1)} %expand.1) | copy-start | bytes 786436
  1.3 4.3 %collective-permute-start = (bf16[4,64,128]{2,1,0:T(8,128)(2,1)S(1)}, bf16[4,64,128]{2,1,0:T(8,128)(2,1)S(1)}, u32[]{:S(2)}, u32[]{:S(2)}) collective-permute-start(bf16[4,64,128]{2,1,0:T(8,128)(2,1)S(1)} %get-tuple-element.15), channel_id=1, source_target_pairs={{0,16},{4,20},{8,24},{12,28},{16,0},{20,4},{24,8},{28,12},{1,17},{... | collective-permute-start | bytes 196616 | tf_op jit(solution)/shard_map/ppermute | solution.py:266
  5.7 0.8 %copy-start.4 = (s32[1024]{0:T(1024)S(1)}, s32[1024]{0:T(1024)}, u32[]{:S(2)}) copy-start(s32[1024]{0:T(1024)} %param.10) | copy-start | bytes 12292
  5.9 4.3 %collective-permute-start.1 = (bf16[4,64,128]{2,1,0:T(8,128)(2,1)S(1)}, bf16[4,64,128]{2,1,0:T(8,128)(2,1)S(1)}, u32[]{:S(2)}, u32[]{:S(2)}) collective-permute-start(bf16[4,64,128]{2,1,0:T(8,128)(2,1)S(1)} %shard_map.92), channel_id=1, source_target_pairs={{0,8},{4,12},{8,0},{12,4},{16,24},{20,28},{24,16},{28,20},{1,9},{5... | collective-permute-start | bytes 196616 | tf_op jit(solution)/shard_map/ppermute | solution.py:266
  8.4 2.0 %copy-start.3 = (bf16[32,1024]{1,0:T(8,128)(2,1)S(1)}, bf16[32,1024]{1,0:T(8,128)(2,1)}, u32[]{:S(2)}) copy-start(bf16[32,1024]{1,0:T(8,128)(2,1)} %points.3) | copy-start | bytes 196612
  8.4 7.7 %copy-start.1 = (bf16[8,3,128,128]{3,2,1,0:T(8,128)(2,1)S(1)}, bf16[8,3,128,128]{3,2,1,0:T(8,128)(2,1)}, u32[]{:S(2)}) copy-start(bf16[8,3,128,128]{3,2,1,0:T(8,128)(2,1)} %dense.1) | copy-start | bytes 2359300
  10.4 6.7 %collective-permute-start.2 = (bf16[4,64,128]{2,1,0:T(8,128)(2,1)S(1)}, bf16[4,64,128]{2,1,0:T(8,128)(2,1)S(1)}, u32[]{:S(2)}, u32[]{:S(2)}) collective-permute-start(bf16[4,64,128]{2,1,0:T(8,128)(2,1)S(1)} %shard_map.95), channel_id=1, source_target_pairs={{0,4},{4,0},{8,12},{12,8},{16,20},{20,16},{24,28},{28,24},{1,5},{5... | collective-permute-start | bytes 196616 | tf_op jit(solution)/shard_map/ppermute | solution.py:266
  10.7 3.8 %collective-permute-start.3 = (bf16[2,32,128]{2,1,0:T(8,128)(2,1)S(1)}, bf16[2,32,128]{2,1,0:T(8,128)(2,1)S(1)}, u32[]{:S(2)}, u32[]{:S(2)}) collective-permute-start(bf16[2,32,128]{2,1,0:T(8,128)(2,1)S(1)} %get-tuple-element.18), channel_id=1, source_target_pairs={{0,1},{1,0},{2,3},{3,2},{4,5},{5,4},{6,7},{7,6},{8,9},{9,8},{10,11... | collective-permute-start | bytes 49160 | tf_op jit(solution)/shard_map/ppermute | solution.py:277
  12.4 3.7 %collective-permute-start.4 = (bf16[2,32,128]{2,1,0:T(8,128)(2,1)S(1)}, bf16[2,32,128]{2,1,0:T(8,128)(2,1)S(1)}, u32[]{:S(2)}, u32[]{:S(2)}) collective-permute-start(bf16[2,32,128]{2,1,0:T(8,128)(2,1)S(1)} %get-tuple-element.20), channel_id=1, source_target_pairs={{0,4},{1,2},{2,1},{3,7},{4,0},{5,6},{6,5},{7,3},{8,12},{9,10},{10,... | collective-permute-start | bytes 49160 | tf_op jit(solution)/shard_map/ppermute | solution.py:277

commit v3 on v2

--- a/solution.py
+++ b/solution.py
@@ -197,7 +197,7 @@
         sent[k] = split(times(received[read(table, places.slot_piece(1, k))], factor[i]))
 
 
-def top_own_body(places, table, received, factor, mixers, own):
+def top_own_body(places, table, received, factor, mixers, dense, own):
     for i in range(own.shape[0]):
         state = split(times(received[read(table, places.piece(0, i))], factor[i]))
         own[i] = times(state, mixers[0, i, 0])
@@ -341,8 +341,8 @@
         [pltpu.SemaphoreType.DMA],
         flops=1 << 24,
     )(order, expand, butterfly_mixers)
-    own = call(part(top_own_body, places), state, [VMEM] * 4, flops=1 << 24)(
-        table, received, top_factor, mixers
+    own = call(part(top_own_body, places), state, [VMEM] * 5, flops=1 << 24)(
+        table, received, top_factor, mixers, nearby_dense_blocks
     )
 
     for level in range(1, levels):

time: 18.4 us -> 18.5 us (level)
  no operation moved by 1% of the time
where the time goes in v3:
time: 18.5 us; the launch traced here: 18.3 us
  waiting for transfers between devices  8.22 us (44%)
  Pallas kernels  6.02 us (33%)
  starting transfers between devices  3.9 us (21%)
    pallas_call x8, Pallas kernels, bound(): run(*[pltpu.with_memory_space_constraint(a, pltpu.HBM) if s is HBM else a...  6.02 us
    ppermute x3, waiting for transfers between devices, from_partner(): return lax.ppermute(x, 'partner', [(i, i ^ 1 << bit) for i in range(count)])  4.49 us
    ppermute x2, waiting for transfers between devices, with_neighbour(): return lax.ppermute(x, ('partner', 'block'), sorted(to.items()))  3.74 us
    ppermute x3, starting transfers between devices, from_partner(): return lax.ppermute(x, 'partner', [(i, i ^ 1 << bit) for i in range(count)])  2.26 us
    ppermute x2, starting transfers between devices, with_neighbour(): return lax.ppermute(x, ('partner', 'block'), sorted(to.items()))  1.64 us
  transfers between devices with their start and end apart: 5, of which 4 were waited for; matrix products, arithmetic and copies ran while one was open for 0% of the time, Pallas kernels for 17%

profile of v3, /device:TPU:18, one launch (start us, length us, event | category | flops | bytes accessed | tf_op | source)
XLA Modules:
  0.0 18.3 jit_solution(78905729005152421)
XLA Ops:
  0.0 0.0 copy-start.1
  0.0 0.0 copy-start.4
  0.0 1.3 %shard_map.91 = (bf16[4,64,128]{2,1,0:T(8,128)(2,1)S(1)}, s32[72,128]{1,0:T(8,128)S(1)}) custom-call(bf16[32,1024]{1,0:T(8,128)(2,1)} %points.3, s32[8,128]{1,0:T(8,128)} %bitcast.2, bf16[8,128,128]{2,1,0:T(8,128)(2,1)} %compress.1, s32[3,8]{1,0:T(4,128)} %block_map.1, s32[3,8]{1,0:T(4,128)} %bitcast.5), custom_call_target="tpu_custom_call" | custom-call | flops 1048576 | bytes 262144 | tf_op jit(solution)/shard_map/pallas_call | solution.py:30
  1.3 0.0 copy-start.2
  1.3 1.6 %collective-permute-start = (bf16[4,64,128]{2,1,0:T(8,128)(2,1)S(1)}, bf16[4,64,128]{2,1,0:T(8,128)(2,1)S(1)}, u32[]{:S(2)}, u32[]{:S(2)}) collective-permute-start(bf16[4,64,128]{2,1,0:T(8,128)(2,1)S(1)} %get-tuple-element.15), channel_id=1, source_target_pairs={{0,16},{4,20},{8,24},{12,28},{16,0},{20,4},{24,8},{28,12},{1,17},{... | collective-permute-start | bytes 196616 | tf_op jit(solution)/shard_map/ppermute | solution.py:266
  2.9 2.7 %collective-permute-done.received = bf16[4,64,128]{2,1,0:T(8,128)(2,1)S(1)} collective-permute-done((bf16[4,64,128]{2,1,0:T(8,128)(2,1)S(1)}, bf16[4,64,128]{2,1,0:T(8,128)(2,1)S(1)}, u32[]{:S(2)}, u32[]{:S(2)}) %collective-permute-start) | collective-permute-done | bytes 65568 | tf_op jit(solution)/shard_map/ppermute | solution.py:266
  5.7 0.0 copy-done.1
  5.7 0.0 copy-start
  5.7 0.2 %shard_map.92 = bf16[4,64,128]{2,1,0:T(8,128)(2,1)S(1)} custom-call(s32[72,128]{1,0:T(8,128)S(1)} %get-tuple-element.14.table, bf16[4,64,128]{2,1,0:T(8,128)(2,1)S(1)} %collective-permute-done.received, bf16[8,128,128]{2,1,0:T(8,128)(2,1)S(1)} %copy-done.1), custom_call_target="tpu_custom_call" | custom-call | flops 1048576 | bytes 262144 | tf_op jit(solution)/shard_map/pallas_call | solution.py:30
  5.9 0.6 %collective-permute-start.1 = (bf16[4,64,128]{2,1,0:T(8,128)(2,1)S(1)}, bf16[4,64,128]{2,1,0:T(8,128)(2,1)S(1)}, u32[]{:S(2)}, u32[]{:S(2)}) collective-permute-start(bf16[4,64,128]{2,1,0:T(8,128)(2,1)S(1)} %shard_map.92), channel_id=1, source_target_pairs={{0,8},{4,12},{8,0},{12,4},{16,24},{20,28},{24,16},{28,20},{1,9},{5... | collective-permute-start | bytes 196616 | tf_op jit(solution)/shard_map/ppermute | solution.py:266
  6.5 0.0 copy-done.4
  6.5 0.0 copy-done.2
  6.5 1.6 %shard_map.93 = (s32[8,1024]{1,0:T(8,128)S(1)}, bf16[8,128,256]{2,1,0:T(8,128)(2,1)S(1)}, bf16[8,128,256]{2,1,0:T(8,128)(2,1)S(1)}, bf16[2,8,2,128,128]{4,3,2,1,0:T(8,128)(2,1)S(1)}) custom-call(s32[8,128]{1,0:T(8,128)S(1)} %bitcast.3, bf16[8,128,128]{2,1,0:T(8,128)(2,1)S(1)} %copy-done.2, bf16[2,8,2,128,128]{4,3,2,1,0:T(8,128)(2,1)} %mixers_in.1), custom_call_target="tpu_custom_call" | custom-call | flops 16777216 | bytes 262144 | tf_op jit(solution)/shard_map/pallas_call | solution.py:30
  8.0 0.0 copy-done
  8.1 0.4 %shard_map.94.own = f32[8,32,128]{2,1,0:T(8,128)S(1)} custom-call(s32[72,128]{1,0:T(8,128)S(1)} %get-tuple-element.14.table, bf16[4,64,128]{2,1,0:T(8,128)(2,1)S(1)} %collective-permute-done.received, bf16[8,128,128]{2,1,0:T(8,128)(2,1)S(1)} %copy-done.1, bf16[2,8,2,128,128]{4,3,2,1,0:T(8,128)(2,1)S(1)} %get-tuple-element.16.mixers, ...), custom_call_target="tpu_custom_call" | custom-call | flops 16777216 | bytes 262144 | tf_op jit(solution)/shard_map/pallas_call | solution.py:30
  8.5 0.0 copy-start.3
  8.5 1.7 %collective-permute-done.1.received = bf16[4,64,128]{2,1,0:T(8,128)(2,1)S(1)} collective-permute-done((bf16[4,64,128]{2,1,0:T(8,128)(2,1)S(1)}, bf16[4,64,128]{2,1,0:T(8,128)(2,1)S(1)}, u32[]{:S(2)}, u32[]{:S(2)}) %collective-permute-start.1) | collective-permute-done | bytes 65568 | tf_op jit(solution)/shard_map/ppermute | solution.py:266
  10.2 0.2 %shard_map.95 = bf16[4,64,128]{2,1,0:T(8,128)(2,1)S(1)} custom-call(s32[72,128]{1,0:T(8,128)S(1)} %get-tuple-element.14.table, bf16[4,64,128]{2,1,0:T(8,128)(2,1)S(1)} %collective-permute-done.1.received, f32[8,32,128]{2,1,0:T(8,128)S(1)} %shard_map.94.own, bf16[2,8,2,128,128]{4,3,2,1,0:T(8,128)(2,1)S(1)} %get-tuple-element.16.mixers), custom_call_target="tpu_custom_call" | custom-call | flops 1048576 | bytes 262144 | tf_op jit(solution)/shard_map/pallas_call | solution.py:30
  10.4 0.1 collective-permute-start.2
  10.5 0.0 copy-done.3
  10.5 0.2 %shard_map.96 = (bf16[8,32,128]{2,1,0:T(8,128)(2,1)S(1)}, bf16[2,32,128]{2,1,0:T(8,128)(2,1)S(1)}, bf16[2,32,128]{2,1,0:T(8,128)(2,1)S(1)}) custom-call(bf16[32,1024]{1,0:T(8,128)(2,1)S(1)} %copy-done.3, s32[8,128]{1,0:T(8,128)S(1)} %bitcast.4), custom_call_target="tpu_custom_call" | custom-call | flops 16777216 | bytes 262144 | tf_op jit(solution)/shard_map/pallas_call | solution.py:30
  10.7 1.6 %collective-permute-start.3 = (bf16[2,32,128]{2,1,0:T(8,128)(2,1)S(1)}, bf16[2,32,128]{2,1,0:T(8,128)(2,1)S(1)}, u32[]{:S(2)}, u32[]{:S(2)}) collective-permute-start(bf16[2,32,128]{2,1,0:T(8,128)(2,1)S(1)} %get-tuple-element.18), channel_id=1, source_target_pairs={{0,1},{1,0},{2,3},{3,2},{4,5},{5,4},{6,7},{7,6},{8,9},{9,8},{10,11... | collective-permute-start | bytes 49160 | tf_op jit(solution)/shard_map/ppermute | solution.py:277
  12.4 0.0 collective-permute-start.4
  12.4 2.2 %collective-permute-done.3.even = bf16[2,32,128]{2,1,0:T(8,128)(2,1)S(1)} collective-permute-done((bf16[2,32,128]{2,1,0:T(8,128)(2,1)S(1)}, bf16[2,32,128]{2,1,0:T(8,128)(2,1)S(1)}, u32[]{:S(2)}, u32[]{:S(2)}) %collective-permute-start.3) | collective-permute-done | bytes 16416 | tf_op jit(solution)/shard_map/ppermute | solution.py:277
  14.5 1.6 %collective-permute-done.4.odd = bf16[2,32,128]{2,1,0:T(8,128)(2,1)S(1)} collective-permute-done((bf16[2,32,128]{2,1,0:T(8,128)(2,1)S(1)}, bf16[2,32,128]{2,1,0:T(8,128)(2,1)S(1)}, u32[]{:S(2)}, u32[]{:S(2)}) %collective-permute-start.4) | collective-permute-done | bytes 16416 | tf_op jit(solution)/shard_map/ppermute | solution.py:277
  16.1 1.0 %shard_map.97.base = f32[8,32,128]{2,1,0:T(8,128)S(1)} custom-call(s32[72,128]{1,0:T(8,128)S(1)} %get-tuple-element.14.table, bf16[4,64,128]{2,1,0:T(8,128)(2,1)S(1)} %collective-permute-done.1.received, f32[8,32,128]{2,1,0:T(8,128)S(1)} %shard_map.94.own, bf16[2,8,2,128,128]{4,3,2,1,0:T(8,128)(2,1)S(1)} %get-tuple-element.16.mixers, ...), custom_call_target="tpu_custom_call" | custom-call | flops 16777216 | bytes 262144 | tf_op jit(solution)/shard_map/pallas_call | solution.py:30
  17.1 0.0 collective-permute-done.2.received
  17.1 1.2 %shard_map.98 = bf16[32,1024]{1,0:T(8,128)(2,1)} custom-call(s32[72,128]{1,0:T(8,128)S(1)} %get-tuple-element.14.table, bf16[4,64,128]{2,1,0:T(8,128)(2,1)S(1)} %collective-permute-done.2.received, f32[8,32,128]{2,1,0:T(8,128)S(1)} %shard_map.97.base, bf16[8,128,256]{2,1,0:T(8,128)(2,1)S(1)} %get-tuple-element.21.joint, s32[8,1024]{1,0:T(8,128)S(1)} %get-tuple-element.22.place), custom_call_target="tpu_custom_call" | custom-call | flops 1048576 | bytes 262144 | tf_op jit(solution)/shard_map/pallas_call | solution.py:30
Async XLA Ops:
  0.0 5.7 %copy-start.1 = (bf16[8,128,128]{2,1,0:T(8,128)(2,1)S(1)}, bf16[8,128,128]{2,1,0:T(8,128)(2,1)}, u32[]{:S(2)}) copy-start(bf16[8,128,128]{2,1,0:T(8,128)(2,1)} %factor.3) | copy-start | bytes 786436
  0.0 6.5 %copy-start.4 = (s32[1024]{0:T(1024)S(1)}, s32[1024]{0:T(1024)}, u32[]{:S(2)}) copy-start(s32[1024]{0:T(1024)} %param.10) | copy-start | bytes 12292
  1.3 5.1 %copy-start.2 = (bf16[8,128,128]{2,1,0:T(8,128)(2,1)S(1)}, bf16[8,128,128]{2,1,0:T(8,128)(2,1)}, u32[]{:S(2)}) copy-start(bf16[8,128,128]{2,1,0:T(8,128)(2,1)} %expand.1) | copy-start | bytes 786436
  1.3 4.3 %collective-permute-start = (bf16[4,64,128]{2,1,0:T(8,128)(2,1)S(1)}, bf16[4,64,128]{2,1,0:T(8,128)(2,1)S(1)}, u32[]{:S(2)}, u32[]{:S(2)}) collective-permute-start(bf16[4,64,128]{2,1,0:T(8,128)(2,1)S(1)} %get-tuple-element.15), channel_id=1, source_target_pairs={{0,16},{4,20},{8,24},{12,28},{16,0},{20,4},{24,8},{28,12},{1,17},{... | collective-permute-start | bytes 196616 | tf_op jit(solution)/shard_map/ppermute | solution.py:266
  5.7 2.4 %copy-start = (bf16[8,3,128,128]{3,2,1,0:T(8,128)(2,1)S(1)}, bf16[8,3,128,128]{3,2,1,0:T(8,128)(2,1)}, u32[]{:S(2)}) copy-start(bf16[8,3,128,128]{3,2,1,0:T(8,128)(2,1)} %dense.3) | copy-start | bytes 2359300
  5.9 4.3 %collective-permute-start.1 = (bf16[4,64,128]{2,1,0:T(8,128)(2,1)S(1)}, bf16[4,64,128]{2,1,0:T(8,128)(2,1)S(1)}, u32[]{:S(2)}, u32[]{:S(2)}) collective-permute-start(bf16[4,64,128]{2,1,0:T(8,128)(2,1)S(1)} %shard_map.92), channel_id=1, source_target_pairs={{0,8},{4,12},{8,0},{12,4},{16,24},{20,28},{24,16},{28,20},{1,9},{5... | collective-permute-start | bytes 196616 | tf_op jit(solution)/shard_map/ppermute | solution.py:266
  8.5 2.0 %copy-start.3 = (bf16[32,1024]{1,0:T(8,128)(2,1)S(1)}, bf16[32,1024]{1,0:T(8,128)(2,1)}, u32[]{:S(2)}) copy-start(bf16[32,1024]{1,0:T(8,128)(2,1)} %points.3) | copy-start | bytes 196612
  10.4 6.7 %collective-permute-start.2 = (bf16[4,64,128]{2,1,0:T(8,128)(2,1)S(1)}, bf16[4,64,128]{2,1,0:T(8,128)(2,1)S(1)}, u32[]{:S(2)}, u32[]{:S(2)}) collective-permute-start(bf16[4,64,128]{2,1,0:T(8,128)(2,1)S(1)} %shard_map.95), channel_id=1, source_target_pairs={{0,4},{4,0},{8,12},{12,8},{16,20},{20,16},{24,28},{28,24},{1,5},{5... | collective-permute-start | bytes 196616 | tf_op jit(solution)/shard_map/ppermute | solution.py:266
  10.7 3.8 %collective-permute-start.3 = (bf16[2,32,128]{2,1,0:T(8,128)(2,1)S(1)}, bf16[2,32,128]{2,1,0:T(8,128)(2,1)S(1)}, u32[]{:S(2)}, u32[]{:S(2)}) collective-permute-start(bf16[2,32,128]{2,1,0:T(8,128)(2,1)S(1)} %get-tuple-element.18), channel_id=1, source_target_pairs={{0,1},{1,0},{2,3},{3,2},{4,5},{5,4},{6,7},{7,6},{8,9},{9,8},{10,11... | collective-permute-start | bytes 49160 | tf_op jit(solution)/shard_map/ppermute | solution.py:277
  12.4 3.7 %collective-permute-start.4 = (bf16[2,32,128]{2,1,0:T(8,128)(2,1)S(1)}, bf16[2,32,128]{2,1,0:T(8,128)(2,1)S(1)}, u32[]{:S(2)}, u32[]{:S(2)}) collective-permute-start(bf16[2,32,128]{2,1,0:T(8,128)(2,1)S(1)} %get-tuple-element.20), channel_id=1, source_target_pairs={{0,4},{1,2},{2,1},{3,7},{4,0},{5,6},{6,5},{7,3},{8,12},{9,10},{10,... | collective-permute-start | bytes 49160 | tf_op jit(solution)/shard_map/ppermute | solution.py:277

commit v4 on v3

--- a/solution.py
+++ b/solution.py
@@ -161,7 +161,8 @@
 
 
 def prep_body(
-    order, expand, mixers_in, place, joint_own, joint, mixers, sem
+    places, table, received, factor, order, expand, mixers_in,
+    own, place, joint_own, joint, mixers, sem,
 ):
     leaves = order.shape[0]
     copy = pltpu.make_async_copy(mixers_in, mixers, sem)
@@ -180,7 +181,12 @@
         )
         total = term if total is None else total + term
     place[...] = total.astype(jnp.int32)
+    states = []
+    for i in range(leaves):
+        states.append(split(times(received[read(table, places.piece(0, i))], factor[i])))
     copy.wait()
+    for i in range(leaves):
+        own[i] = times(states[i], mixers[0, i, 0])
     for side, out in enumerate((joint_own, joint)):
         for i in range(leaves):
             both = jnp.dot(
@@ -197,13 +203,7 @@
         sent[k] = split(times(received[read(table, places.slot_piece(1, k))], factor[i]))
 
 
-def top_own_body(places, table, received, factor, mixers, dense, own):
-    for i in range(own.shape[0]):
-        state = split(times(received[read(table, places.piece(0, i))], factor[i]))
-        own[i] = times(state, mixers[0, i, 0])
-
-
-def mix_send_body(places, level, table, received, own, mixers, sent):
+def mix_send_body(places, level, table, received, own, mixers, dense, sent):
     for k in range(sent.shape[0]):
         i = read(table, places.slot(level + 1, k))
         piece = received[read(table, places.slot_piece(level + 1, k))]
@@ -329,27 +329,25 @@
 
     sent = call(part(top_send_body, places), pair, [VMEM] * 3)(table, received, top_factor)
     wide = jax.ShapeDtypeStruct((leaves, LANES, 2 * LANES), jnp.bfloat16)
-    place, joint_own, joint, mixers = call(
-        prep_body,
+    own, place, joint_own, joint, mixers = call(
+        part(prep_body, places),
         [
+            state,
             jax.ShapeDtypeStruct((8, count), jnp.int32),
             wide,
             wide,
             jax.ShapeDtypeStruct(butterfly_mixers.shape, butterfly_mixers.dtype),
         ],
-        [VMEM, VMEM, HBM],
+        [VMEM] * 5 + [HBM],
         [pltpu.SemaphoreType.DMA],
         flops=1 << 24,
-    )(order, expand, butterfly_mixers)
-    own = call(part(top_own_body, places), state, [VMEM] * 5, flops=1 << 24)(
-        table, received, top_factor, mixers, nearby_dense_blocks
-    )
+    )(table, received, top_factor, order, expand, butterfly_mixers)
 
     for level in range(1, levels):
         received = from_partner(sent, levels - 1 - level)
         if level < levels - 1:
-            sent = call(part(mix_send_body, places, level), pair, [VMEM] * 4)(
-                table, received, own, mixers
+            sent = call(part(mix_send_body, places, level), pair, [VMEM] * 5)(
+                table, received, own, mixers, nearby_dense_blocks
             )
             if level < levels - 2:
                 body, factors, scratch = mix_own_body, (mixers,), ()

time: 18.5 us -> 19 us (1.027)
  local copies, waits for them, and re-layouts: 0.02 us -> 0.58 us
  Pallas kernels: 6.02 us -> 6.24 us
  waiting for transfers between devices: 8.22 us -> 8.02 us
    unnamed x10, local copies, waits for them, and re-layouts: 0.02 us -> 0.58 us
    pallas_call x8 -> x7, Pallas kernels: 6.02 us -> 6.24 us  [bound(): run(*[pltpu.with_memory_space_constraint(a, pltpu.HBM) if s is HBM else a...]
    ppermute x3, waiting for transfers between devices: 4.49 us -> 4.28 us  [from_partner(): return lax.ppermute(x, 'partner', [(i, i ^ 1 << bit) for i in range(count)])]
  transfers between devices with their start and end apart: 5 -> 5, of which waited for: 4 -> 4; matrix products, arithmetic and copies ran while one was open for 0% -> 0% of each run, Pallas kernels for 17% -> 18%
where the time goes in v4:
time: 19 us; the launch traced here: 18.8 us
  waiting for transfers between devices  8.02 us (42%)
  Pallas kernels  6.24 us (33%)
  starting transfers between devices  3.9 us (21%)
  local copies, waits for them, and re-layouts  0.58 us (3%)
    pallas_call x7, Pallas kernels, bound(): run(*[pltpu.with_memory_space_constraint(a, pltpu.HBM) if s is HBM else a...  6.24 us
    ppermute x3, waiting for transfers between devices, from_partner(): return lax.ppermute(x, 'partner', [(i, i ^ 1 << bit) for i in range(count)])  4.28 us
    ppermute x2, waiting for transfers between devices, with_neighbour(): return lax.ppermute(x, ('partner', 'block'), sorted(to.items()))  3.74 us
    ppermute x3, starting transfers between devices, from_partner(): return lax.ppermute(x, 'partner', [(i, i ^ 1 << bit) for i in range(count)])  2.26 us
    ppermute x2, starting transfers between devices, with_neighbour(): return lax.ppermute(x, ('partner', 'block'), sorted(to.items()))  1.64 us
    unnamed x10, local copies, waits for them, and re-layouts  0.58 us
  transfers between devices with their start and end apart: 5, of which 4 were waited for; matrix products, arithmetic and copies ran while one was open for 0% of the time, Pallas kernels for 18%

profile of v4, /device:TPU:18, one launch (start us, length us, event | category | flops | bytes accessed | tf_op | source)
XLA Modules:
  0.0 18.8 jit_solution(17989400549060267858)
XLA Ops:
  0.0 0.0 copy-start.1
  0.0 1.3 %shard_map.91 = (bf16[4,64,128]{2,1,0:T(8,128)(2,1)S(1)}, s32[72,128]{1,0:T(8,128)S(1)}) custom-call(bf16[32,1024]{1,0:T(8,128)(2,1)} %points.3, s32[8,128]{1,0:T(8,128)} %bitcast.2, bf16[8,128,128]{2,1,0:T(8,128)(2,1)} %compress.1, s32[3,8]{1,0:T(4,128)} %block_map.1, s32[3,8]{1,0:T(4,128)} %bitcast.5), custom_call_target="tpu_custom_call" | custom-call | flops 1048576 | bytes 262144 | tf_op jit(solution)/shard_map/pallas_call | solution.py:30
  1.3 0.0 copy-start.2
  1.3 1.6 %collective-permute-start = (bf16[4,64,128]{2,1,0:T(8,128)(2,1)S(1)}, bf16[4,64,128]{2,1,0:T(8,128)(2,1)S(1)}, u32[]{:S(2)}, u32[]{:S(2)}) collective-permute-start(bf16[4,64,128]{2,1,0:T(8,128)(2,1)S(1)} %get-tuple-element.16), channel_id=1, source_target_pairs={{0,16},{4,20},{8,24},{12,28},{16,0},{20,4},{24,8},{28,12},{1,17},{... | collective-permute-start | bytes 196616 | tf_op jit(solution)/shard_map/ppermute | solution.py:266
  2.9 2.7 %collective-permute-done.received = bf16[4,64,128]{2,1,0:T(8,128)(2,1)S(1)} collective-permute-done((bf16[4,64,128]{2,1,0:T(8,128)(2,1)S(1)}, bf16[4,64,128]{2,1,0:T(8,128)(2,1)S(1)}, u32[]{:S(2)}, u32[]{:S(2)}) %collective-permute-start) | collective-permute-done | bytes 65568 | tf_op jit(solution)/shard_map/ppermute | solution.py:266
  5.7 0.0 copy-done.1
  5.7 0.0 copy-start.4
  5.7 0.2 shard_map.92
  5.9 0.0 copy-start
  5.9 0.6 %collective-permute-start.1 = (bf16[4,64,128]{2,1,0:T(8,128)(2,1)S(1)}, bf16[4,64,128]{2,1,0:T(8,128)(2,1)S(1)}, u32[]{:S(2)}, u32[]{:S(2)}) collective-permute-start(bf16[4,64,128]{2,1,0:T(8,128)(2,1)S(1)} %shard_map.92), channel_id=1, source_target_pairs={{0,8},{4,12},{8,0},{12,4},{16,24},{20,28},{24,16},{28,20},{1,9},{5... | collective-permute-start | bytes 196616 | tf_op jit(solution)/shard_map/ppermute | solution.py:266
  6.5 0.0 copy-done.2
  6.5 0.0 copy-done.4
  6.5 2.2 %shard_map.93 = (f32[8,32,128]{2,1,0:T(8,128)S(1)}, s32[8,1024]{1,0:T(8,128)S(1)}, bf16[8,128,256]{2,1,0:T(8,128)(2,1)S(1)}, bf16[8,128,256]{2,1,0:T(8,128)(2,1)S(1)}, bf16[2,8,2,128,128]{4,3,2,1,0:T(8,128)(2,1)S(1)}) custom-call(s32[72,128]{1,0:T(8,128)S(1)} %get-tuple-element.15.table, bf16[4,64,128]{2,1,0:T(8,128)(2,1)S(1)} %collective-permute-done.received, ...), custom_call_target="tpu_custom_call" | custom-call | flops 16777216 | bytes 262144 | tf_op jit(solution)/shard_map/pallas_call | solution.py:30
  8.7 1.5 %collective-permute-done.1.received = bf16[4,64,128]{2,1,0:T(8,128)(2,1)S(1)} collective-permute-done((bf16[4,64,128]{2,1,0:T(8,128)(2,1)S(1)}, bf16[4,64,128]{2,1,0:T(8,128)(2,1)S(1)}, u32[]{:S(2)}, u32[]{:S(2)}) %collective-permute-start.1) | collective-permute-done | bytes 65568 | tf_op jit(solution)/shard_map/ppermute | solution.py:266
  10.2 0.0 copy-done
  10.2 0.0 copy-start.3
  10.2 0.2 shard_map.94
  10.4 0.1 collective-permute-start.2
  10.5 0.6 %copy-done.3 = bf16[32,1024]{1,0:T(8,128)(2,1)S(1)} copy-done((bf16[32,1024]{1,0:T(8,128)(2,1)S(1)}, bf16[32,1024]{1,0:T(8,128)(2,1)}, u32[]{:S(2)}) %copy-start.3) | copy-done | bytes 65560
  11.1 0.2 %shard_map.95 = (bf16[8,32,128]{2,1,0:T(8,128)(2,1)S(1)}, bf16[2,32,128]{2,1,0:T(8,128)(2,1)S(1)}, bf16[2,32,128]{2,1,0:T(8,128)(2,1)S(1)}) custom-call(bf16[32,1024]{1,0:T(8,128)(2,1)S(1)} %copy-done.3, s32[8,128]{1,0:T(8,128)S(1)} %bitcast.4), custom_call_target="tpu_custom_call" | custom-call | flops 16777216 | bytes 262144 | tf_op jit(solution)/shard_map/pallas_call | solution.py:30
  11.3 1.6 %collective-permute-start.3 = (bf16[2,32,128]{2,1,0:T(8,128)(2,1)S(1)}, bf16[2,32,128]{2,1,0:T(8,128)(2,1)S(1)}, u32[]{:S(2)}, u32[]{:S(2)}) collective-permute-start(bf16[2,32,128]{2,1,0:T(8,128)(2,1)S(1)} %get-tuple-element.20), channel_id=1, source_target_pairs={{0,1},{1,0},{2,3},{3,2},{4,5},{5,4},{6,7},{7,6},{8,9},{9,8},{10,11... | collective-permute-start | bytes 49160 | tf_op jit(solution)/shard_map/ppermute | solution.py:277
  12.9 0.0 collective-permute-start.4
  12.9 2.2 %collective-permute-done.3.even = bf16[2,32,128]{2,1,0:T(8,128)(2,1)S(1)} collective-permute-done((bf16[2,32,128]{2,1,0:T(8,128)(2,1)S(1)}, bf16[2,32,128]{2,1,0:T(8,128)(2,1)S(1)}, u32[]{:S(2)}, u32[]{:S(2)}) %collective-permute-start.3) | collective-permute-done | bytes 16416 | tf_op jit(solution)/shard_map/ppermute | solution.py:277
  15.1 1.6 %collective-permute-done.4.odd = bf16[2,32,128]{2,1,0:T(8,128)(2,1)S(1)} collective-permute-done((bf16[2,32,128]{2,1,0:T(8,128)(2,1)S(1)}, bf16[2,32,128]{2,1,0:T(8,128)(2,1)S(1)}, u32[]{:S(2)}, u32[]{:S(2)}) %collective-permute-start.4) | collective-permute-done | bytes 16416 | tf_op jit(solution)/shard_map/ppermute | solution.py:277
  16.7 1.0 %shard_map.96.base = f32[8,32,128]{2,1,0:T(8,128)S(1)} custom-call(s32[72,128]{1,0:T(8,128)S(1)} %get-tuple-element.15.table, bf16[4,64,128]{2,1,0:T(8,128)(2,1)S(1)} %collective-permute-done.1.received, f32[8,32,128]{2,1,0:T(8,128)S(1)} %get-tuple-element.17.own, bf16[2,8,2,128,128]{4,3,2,1,0:T(8,128)(2,1)S(1)} %get-tuple-element.18.mixers, ...), custom_call_target="tpu_custom_call" | custom-call | flops 16777216 | bytes 262144 | tf_op jit(solution)/shard_map/pallas_call | solution.py:30
  17.6 0.0 collective-permute-done.2.received
  17.6 1.2 %shard_map.97 = bf16[32,1024]{1,0:T(8,128)(2,1)} custom-call(s32[72,128]{1,0:T(8,128)S(1)} %get-tuple-element.15.table, bf16[4,64,128]{2,1,0:T(8,128)(2,1)S(1)} %collective-permute-done.2.received, f32[8,32,128]{2,1,0:T(8,128)S(1)} %shard_map.96.base, bf16[8,128,256]{2,1,0:T(8,128)(2,1)S(1)} %get-tuple-element.23.joint, s32[8,1024]{1,0:T(8,128)S(1)} %get-tuple-element.24.place), custom_call_target="tpu_custom_call" | custom-call | flops 1048576 | bytes 262144 | tf_op jit(solution)/shard_map/pallas_call | solution.py:30
Async XLA Ops:
  0.0 5.7 %copy-start.1 = (bf16[8,128,128]{2,1,0:T(8,128)(2,1)S(1)}, bf16[8,128,128]{2,1,0:T(8,128)(2,1)}, u32[]{:S(2)}) copy-start(bf16[8,128,128]{2,1,0:T(8,128)(2,1)} %factor.3) | copy-start | bytes 786436
  1.3 5.2 %copy-start.2 = (bf16[8,128,128]{2,1,0:T(8,128)(2,1)S(1)}, bf16[8,128,128]{2,1,0:T(8,128)(2,1)}, u32[]{:S(2)}) copy-start(bf16[8,128,128]{2,1,0:T(8,128)(2,1)} %expand.1) | copy-start | bytes 786436
  1.3 4.3 %collective-permute-start = (bf16[4,64,128]{2,1,0:T(8,128)(2,1)S(1)}, bf16[4,64,128]{2,1,0:T(8,128)(2,1)S(1)}, u32[]{:S(2)}, u32[]{:S(2)}) collective-permute-start(bf16[4,64,128]{2,1,0:T(8,128)(2,1)S(1)} %get-tuple-element.16), channel_id=1, source_target_pairs={{0,16},{4,20},{8,24},{12,28},{16,0},{20,4},{24,8},{28,12},{1,17},{... | collective-permute-start | bytes 196616 | tf_op jit(solution)/shard_map/ppermute | solution.py:266
  5.7 0.8 %copy-start.4 = (s32[1024]{0:T(1024)S(1)}, s32[1024]{0:T(1024)}, u32[]{:S(2)}) copy-start(s32[1024]{0:T(1024)} %param.10) | copy-start | bytes 12292
  5.9 4.4 %copy-start = (bf16[8,3,128,128]{3,2,1,0:T(8,128)(2,1)S(1)}, bf16[8,3,128,128]{3,2,1,0:T(8,128)(2,1)}, u32[]{:S(2)}) copy-start(bf16[8,3,128,128]{3,2,1,0:T(8,128)(2,1)} %dense.3) | copy-start | bytes 2359300
  5.9 4.3 %collective-permute-start.1 = (bf16[4,64,128]{2,1,0:T(8,128)(2,1)S(1)}, bf16[4,64,128]{2,1,0:T(8,128)(2,1)S(1)}, u32[]{:S(2)}, u32[]{:S(2)}) collective-permute-start(bf16[4,64,128]{2,1,0:T(8,128)(2,1)S(1)} %shard_map.92), channel_id=1, source_target_pairs={{0,8},{4,12},{8,0},{12,4},{16,24},{20,28},{24,16},{28,20},{1,9},{5... | collective-permute-start | bytes 196616 | tf_op jit(solution)/shard_map/ppermute | solution.py:266
  10.2 0.8 %copy-start.3 = (bf16[32,1024]{1,0:T(8,128)(2,1)S(1)}, bf16[32,1024]{1,0:T(8,128)(2,1)}, u32[]{:S(2)}) copy-start(bf16[32,1024]{1,0:T(8,128)(2,1)} %points.3) | copy-start | bytes 196612
  10.4 7.2 %collective-permute-start.2 = (bf16[4,64,128]{2,1,0:T(8,128)(2,1)S(1)}, bf16[4,64,128]{2,1,0:T(8,128)(2,1)S(1)}, u32[]{:S(2)}, u32[]{:S(2)}) collective-permute-start(bf16[4,64,128]{2,1,0:T(8,128)(2,1)S(1)} %shard_map.94), channel_id=1, source_target_pairs={{0,4},{4,0},{8,12},{12,8},{16,20},{20,16},{24,28},{28,24},{1,5},{5... | collective-permute-start | bytes 196616 | tf_op jit(solution)/shard_map/ppermute | solution.py:266
  11.3 3.8 %collective-permute-start.3 = (bf16[2,32,128]{2,1,0:T(8,128)(2,1)S(1)}, bf16[2,32,128]{2,1,0:T(8,128)(2,1)S(1)}, u32[]{:S(2)}, u32[]{:S(2)}) collective-permute-start(bf16[2,32,128]{2,1,0:T(8,128)(2,1)S(1)} %get-tuple-element.20), channel_id=1, source_target_pairs={{0,1},{1,0},{2,3},{3,2},{4,5},{5,4},{6,7},{7,6},{8,9},{9,8},{10,11... | collective-permute-start | bytes 49160 | tf_op jit(solution)/shard_map/ppermute | solution.py:277
  12.9 3.7 %collective-permute-start.4 = (bf16[2,32,128]{2,1,0:T(8,128)(2,1)S(1)}, bf16[2,32,128]{2,1,0:T(8,128)(2,1)S(1)}, u32[]{:S(2)}, u32[]{:S(2)}) collective-permute-start(bf16[2,32,128]{2,1,0:T(8,128)(2,1)S(1)} %get-tuple-element.22), channel_id=1, source_target_pairs={{0,4},{1,2},{2,1},{3,7},{4,0},{5,6},{6,5},{7,3},{8,12},{9,10},{10,... | collective-permute-start | bytes 49160 | tf_op jit(solution)/shard_map/ppermute | solution.py:277

commit v5 on v3

--- a/solution.py
+++ b/solution.py
@@ -161,11 +161,17 @@
 
 
 def prep_body(
-    order, expand, mixers_in, place, joint_own, joint, mixers, sem
+    order, expand, mixers_in, place, joint_own, joint, mixers, sems
 ):
     leaves = order.shape[0]
-    copy = pltpu.make_async_copy(mixers_in, mixers, sem)
-    copy.start()
+    levels = mixers.shape[0]
+    tail, rest = pl.ds(levels - 1, 1), pl.ds(0, levels - 1)
+    copies = [
+        pltpu.make_async_copy(mixers_in.at[part], mixers.at[part], sems.at[i])
+        for i, part in enumerate((tail, rest))
+    ]
+    for copy in copies:
+        copy.start()
     count = leaves * LANES
     target = lax.broadcasted_iota(jnp.int32, (count, LANES), 0)
     kind = lax.broadcasted_iota(jnp.int32, (8, LANES), 0)
@@ -180,7 +186,7 @@
         )
         total = term if total is None else total + term
     place[...] = total.astype(jnp.int32)
-    copy.wait()
+    copies[0].wait()
     for side, out in enumerate((joint_own, joint)):
         for i in range(leaves):
             both = jnp.dot(
@@ -189,6 +195,7 @@
             high = both.astype(jnp.bfloat16)
             out[i, :, :LANES] = high
             out[i, :, LANES:] = (both - high.astype(jnp.float32)).astype(jnp.bfloat16)
+    copies[1].wait()
 
 
 def top_send_body(places, table, received, factor, sent):
@@ -234,10 +241,11 @@
     for i in range(leaves):
         other = times(received[read(table, places.piece(level, i))], mixers[level - 1, i, 1])
         total = times_joint(split(own[i] + other), joint_own[i])
-        for n in range(near_count):
-            source = windows[read(table, places.near(i, n))]
-            total = total + jnp.dot(source, dense[i, n], preferred_element_type=jnp.float32)
-        base[i] = total
+        source = jnp.concatenate(
+            [windows[read(table, places.near(i, n))] for n in range(near_count)], axis=1
+        )
+        factor = dense[i].reshape(near_count * LANES, LANES)
+        base[i] = total + jnp.dot(source, factor, preferred_element_type=jnp.float32)
 
 
 def last_body(places, level, table, received, base, joint, place, applied, rows, sems):
@@ -338,7 +346,7 @@
             jax.ShapeDtypeStruct(butterfly_mixers.shape, butterfly_mixers.dtype),
         ],
         [VMEM, VMEM, HBM],
-        [pltpu.SemaphoreType.DMA],
+        [pltpu.SemaphoreType.DMA((2,))],
         flops=1 << 24,
     )(order, expand, butterfly_mixers)
     own = call(part(top_own_body, places), state, [VMEM] * 5, flops=1 << 24)(

time: 18.5 us -> 18.1 us (0.978)
  the two profiles are of different devices: /device:TPU:18 before, /device:TPU:22 now
where the time goes in v5:
time: 18.1 us; the launch traced here: 17.9 us
  waiting for transfers between devices  9.41 us (52%)
  Pallas kernels  5.46 us (30%)
  starting transfers between devices  2.89 us (16%)
    ppermute x3, waiting for transfers between devices, from_partner(): return lax.ppermute(x, 'partner', [(i, i ^ 1 << bit) for i in range(count)])  5.67 us
    pallas_call x8, Pallas kernels, bound(): run(*[pltpu.with_memory_space_constraint(a, pltpu.HBM) if s is HBM else a...  5.46 us
    ppermute x2, waiting for transfers between devices, with_neighbour(): return lax.ppermute(x, ('partner', 'block'), sorted(to.items()))  3.74 us
    ppermute x2, starting transfers between devices, with_neighbour(): return lax.ppermute(x, ('partner', 'block'), sorted(to.items()))  1.64 us
    ppermute x3, starting transfers between devices, from_partner(): return lax.ppermute(x, 'partner', [(i, i ^ 1 << bit) for i in range(count)])  1.25 us
  transfers between devices with their start and end apart: 5, of which 4 were waited for; matrix products, arithmetic and copies ran while one was open for 0% of the time, Pallas kernels for 15%

profile of v5, /device:TPU:22, one launch (start us, length us, event | category | flops | bytes accessed | tf_op | source)
XLA Modules:
  0.0 17.9 jit_solution(17896362443259294601)
XLA Ops:
  0.0 0.0 copy-start.1
  0.0 0.0 copy-start.4
  0.0 1.3 %shard_map.91 = (bf16[4,64,128]{2,1,0:T(8,128)(2,1)S(1)}, s32[72,128]{1,0:T(8,128)S(1)}) custom-call(bf16[32,1024]{1,0:T(8,128)(2,1)} %points.3, s32[8,128]{1,0:T(8,128)} %bitcast.2, bf16[8,128,128]{2,1,0:T(8,128)(2,1)} %compress.1, s32[3,8]{1,0:T(4,128)} %block_map.1, s32[3,8]{1,0:T(4,128)} %bitcast.5), custom_call_target="tpu_custom_call" | custom-call | flops 1048576 | bytes 262144 | tf_op jit(solution)/shard_map/pallas_call | solution.py:30
  1.3 0.0 copy-start.2
  1.3 0.6 %collective-permute-start = (bf16[4,64,128]{2,1,0:T(8,128)(2,1)S(1)}, bf16[4,64,128]{2,1,0:T(8,128)(2,1)S(1)}, u32[]{:S(2)}, u32[]{:S(2)}) collective-permute-start(bf16[4,64,128]{2,1,0:T(8,128)(2,1)S(1)} %get-tuple-element.15), channel_id=1, source_target_pairs={{0,16},{4,20},{8,24},{12,28},{16,0},{20,4},{24,8},{28,12},{1,17},{... | collective-permute-start | bytes 196616 | tf_op jit(solution)/shard_map/ppermute | solution.py:274
  1.9 3.8 %collective-permute-done.received = bf16[4,64,128]{2,1,0:T(8,128)(2,1)S(1)} collective-permute-done((bf16[4,64,128]{2,1,0:T(8,128)(2,1)S(1)}, bf16[4,64,128]{2,1,0:T(8,128)(2,1)S(1)}, u32[]{:S(2)}, u32[]{:S(2)}) %collective-permute-start) | collective-permute-done | bytes 65568 | tf_op jit(solution)/shard_map/ppermute | solution.py:274
  5.7 0.0 copy-done.1
  5.7 0.0 copy-start
  5.7 0.2 %shard_map.92 = bf16[4,64,128]{2,1,0:T(8,128)(2,1)S(1)} custom-call(s32[72,128]{1,0:T(8,128)S(1)} %get-tuple-element.14.table, bf16[4,64,128]{2,1,0:T(8,128)(2,1)S(1)} %collective-permute-done.received, bf16[8,128,128]{2,1,0:T(8,128)(2,1)S(1)} %copy-done.1), custom_call_target="tpu_custom_call" | custom-call | flops 1048576 | bytes 262144 | tf_op jit(solution)/shard_map/pallas_call | solution.py:30
  5.9 0.6 %collective-permute-start.1 = (bf16[4,64,128]{2,1,0:T(8,128)(2,1)S(1)}, bf16[4,64,128]{2,1,0:T(8,128)(2,1)S(1)}, u32[]{:S(2)}, u32[]{:S(2)}) collective-permute-start(bf16[4,64,128]{2,1,0:T(8,128)(2,1)S(1)} %shard_map.92), channel_id=1, source_target_pairs={{0,8},{4,12},{8,0},{12,4},{16,24},{20,28},{24,16},{28,20},{1,9},{5... | collective-permute-start | bytes 196616 | tf_op jit(solution)/shard_map/ppermute | solution.py:274
  6.5 0.0 copy-done.4
  6.5 0.0 copy-done.2
  6.5 1.4 %shard_map.93 = (s32[8,1024]{1,0:T(8,128)S(1)}, bf16[8,128,256]{2,1,0:T(8,128)(2,1)S(1)}, bf16[8,128,256]{2,1,0:T(8,128)(2,1)S(1)}, bf16[2,8,2,128,128]{4,3,2,1,0:T(8,128)(2,1)S(1)}) custom-call(s32[8,128]{1,0:T(8,128)S(1)} %bitcast.3, bf16[8,128,128]{2,1,0:T(8,128)(2,1)S(1)} %copy-done.2, bf16[2,8,2,128,128]{4,3,2,1,0:T(8,128)(2,1)} %mixers_in.1), custom_call_target="tpu_custom_call" | custom-call | flops 16777216 | bytes 262144 | tf_op jit(solution)/shard_map/pallas_call | solution.py:30
  7.9 0.0 copy-done
  7.9 0.4 %shard_map.94.own = f32[8,32,128]{2,1,0:T(8,128)S(1)} custom-call(s32[72,128]{1,0:T(8,128)S(1)} %get-tuple-element.14.table, bf16[4,64,128]{2,1,0:T(8,128)(2,1)S(1)} %collective-permute-done.received, bf16[8,128,128]{2,1,0:T(8,128)(2,1)S(1)} %copy-done.1, bf16[2,8,2,128,128]{4,3,2,1,0:T(8,128)(2,1)S(1)} %get-tuple-element.16.mixers, ...), custom_call_target="tpu_custom_call" | custom-call | flops 16777216 | bytes 262144 | tf_op jit(solution)/shard_map/pallas_call | solution.py:30
  8.3 0.0 copy-start.3
  8.3 1.9 %collective-permute-done.1.received = bf16[4,64,128]{2,1,0:T(8,128)(2,1)S(1)} collective-permute-done((bf16[4,64,128]{2,1,0:T(8,128)(2,1)S(1)}, bf16[4,64,128]{2,1,0:T(8,128)(2,1)S(1)}, u32[]{:S(2)}, u32[]{:S(2)}) %collective-permute-start.1) | collective-permute-done | bytes 65568 | tf_op jit(solution)/shard_map/ppermute | solution.py:274
  10.2 0.2 %shard_map.95 = bf16[4,64,128]{2,1,0:T(8,128)(2,1)S(1)} custom-call(s32[72,128]{1,0:T(8,128)S(1)} %get-tuple-element.14.table, bf16[4,64,128]{2,1,0:T(8,128)(2,1)S(1)} %collective-permute-done.1.received, f32[8,32,128]{2,1,0:T(8,128)S(1)} %shard_map.94.own, bf16[2,8,2,128,128]{4,3,2,1,0:T(8,128)(2,1)S(1)} %get-tuple-element.16.mixers), custom_call_target="tpu_custom_call" | custom-call | flops 1048576 | bytes 262144 | tf_op jit(solution)/shard_map/pallas_call | solution.py:30
  10.4 0.1 collective-permute-start.2
  10.5 0.0 copy-done.3
  10.5 0.2 %shard_map.96 = (bf16[8,32,128]{2,1,0:T(8,128)(2,1)S(1)}, bf16[2,32,128]{2,1,0:T(8,128)(2,1)S(1)}, bf16[2,32,128]{2,1,0:T(8,128)(2,1)S(1)}) custom-call(bf16[32,1024]{1,0:T(8,128)(2,1)S(1)} %copy-done.3, s32[8,128]{1,0:T(8,128)S(1)} %bitcast.4), custom_call_target="tpu_custom_call" | custom-call | flops 16777216 | bytes 262144 | tf_op jit(solution)/shard_map/pallas_call | solution.py:30
  10.7 1.6 %collective-permute-start.3 = (bf16[2,32,128]{2,1,0:T(8,128)(2,1)S(1)}, bf16[2,32,128]{2,1,0:T(8,128)(2,1)S(1)}, u32[]{:S(2)}, u32[]{:S(2)}) collective-permute-start(bf16[2,32,128]{2,1,0:T(8,128)(2,1)S(1)} %get-tuple-element.18), channel_id=1, source_target_pairs={{0,1},{1,0},{2,3},{3,2},{4,5},{5,4},{6,7},{7,6},{8,9},{9,8},{10,11... | collective-permute-start | bytes 49160 | tf_op jit(solution)/shard_map/ppermute | solution.py:285
  12.4 0.0 collective-permute-start.4
  12.4 2.2 %collective-permute-done.3.even = bf16[2,32,128]{2,1,0:T(8,128)(2,1)S(1)} collective-permute-done((bf16[2,32,128]{2,1,0:T(8,128)(2,1)S(1)}, bf16[2,32,128]{2,1,0:T(8,128)(2,1)S(1)}, u32[]{:S(2)}, u32[]{:S(2)}) %collective-permute-start.3) | collective-permute-done | bytes 16416 | tf_op jit(solution)/shard_map/ppermute | solution.py:285
  14.5 1.6 %collective-permute-done.4.odd = bf16[2,32,128]{2,1,0:T(8,128)(2,1)S(1)} collective-permute-done((bf16[2,32,128]{2,1,0:T(8,128)(2,1)S(1)}, bf16[2,32,128]{2,1,0:T(8,128)(2,1)S(1)}, u32[]{:S(2)}, u32[]{:S(2)}) %collective-permute-start.4) | collective-permute-done | bytes 16416 | tf_op jit(solution)/shard_map/ppermute | solution.py:285
  16.1 0.6 %shard_map.97.base = f32[8,32,128]{2,1,0:T(8,128)S(1)} custom-call(s32[72,128]{1,0:T(8,128)S(1)} %get-tuple-element.14.table, bf16[4,64,128]{2,1,0:T(8,128)(2,1)S(1)} %collective-permute-done.1.received, f32[8,32,128]{2,1,0:T(8,128)S(1)} %shard_map.94.own, bf16[2,8,2,128,128]{4,3,2,1,0:T(8,128)(2,1)S(1)} %get-tuple-element.16.mixers, ...), custom_call_target="tpu_custom_call" | custom-call | flops 16777216 | bytes 262144 | tf_op jit(solution)/shard_map/pallas_call | solution.py:30
  16.7 0.0 collective-permute-done.2.received
  16.7 1.2 %shard_map.98 = bf16[32,1024]{1,0:T(8,128)(2,1)} custom-call(s32[72,128]{1,0:T(8,128)S(1)} %get-tuple-element.14.table, bf16[4,64,128]{2,1,0:T(8,128)(2,1)S(1)} %collective-permute-done.2.received, f32[8,32,128]{2,1,0:T(8,128)S(1)} %shard_map.97.base, bf16[8,128,256]{2,1,0:T(8,128)(2,1)S(1)} %get-tuple-element.21.joint, s32[8,1024]{1,0:T(8,128)S(1)} %get-tuple-element.22.place), custom_call_target="tpu_custom_call" | custom-call | flops 1048576 | bytes 262144 | tf_op jit(solution)/shard_map/pallas_call | solution.py:30
Async XLA Ops:
  0.0 5.7 %copy-start.1 = (bf16[8,128,128]{2,1,0:T(8,128)(2,1)S(1)}, bf16[8,128,128]{2,1,0:T(8,128)(2,1)}, u32[]{:S(2)}) copy-start(bf16[8,128,128]{2,1,0:T(8,128)(2,1)} %factor.3) | copy-start | bytes 786436
  0.0 6.5 %copy-start.4 = (s32[1024]{0:T(1024)S(1)}, s32[1024]{0:T(1024)}, u32[]{:S(2)}) copy-start(s32[1024]{0:T(1024)} %param.10) | copy-start | bytes 12292
  1.3 5.1 %copy-start.2 = (bf16[8,128,128]{2,1,0:T(8,128)(2,1)S(1)}, bf16[8,128,128]{2,1,0:T(8,128)(2,1)}, u32[]{:S(2)}) copy-start(bf16[8,128,128]{2,1,0:T(8,128)(2,1)} %expand.1) | copy-start | bytes 786436
  1.3 4.3 %collective-permute-start = (bf16[4,64,128]{2,1,0:T(8,128)(2,1)S(1)}, bf16[4,64,128]{2,1,0:T(8,128)(2,1)S(1)}, u32[]{:S(2)}, u32[]{:S(2)}) collective-permute-start(bf16[4,64,128]{2,1,0:T(8,128)(2,1)S(1)} %get-tuple-element.15), channel_id=1, source_target_pairs={{0,16},{4,20},{8,24},{12,28},{16,0},{20,4},{24,8},{28,12},{1,17},{... | collective-permute-start | bytes 196616 | tf_op jit(solution)/shard_map/ppermute | solution.py:274
  5.7 2.2 %copy-start = (bf16[8,3,128,128]{3,2,1,0:T(8,128)(2,1)S(1)}, bf16[8,3,128,128]{3,2,1,0:T(8,128)(2,1)}, u32[]{:S(2)}) copy-start(bf16[8,3,128,128]{3,2,1,0:T(8,128)(2,1)} %dense.3) | copy-start | bytes 2359300
  5.9 4.3 %collective-permute-start.1 = (bf16[4,64,128]{2,1,0:T(8,128)(2,1)S(1)}, bf16[4,64,128]{2,1,0:T(8,128)(2,1)S(1)}, u32[]{:S(2)}, u32[]{:S(2)}) collective-permute-start(bf16[4,64,128]{2,1,0:T(8,128)(2,1)S(1)} %shard_map.92), channel_id=1, source_target_pairs={{0,8},{4,12},{8,0},{12,4},{16,24},{20,28},{24,16},{28,20},{1,9},{5... | collective-permute-start | bytes 196616 | tf_op jit(solution)/shard_map/ppermute | solution.py:274
  8.3 2.2 %copy-start.3 = (bf16[32,1024]{1,0:T(8,128)(2,1)S(1)}, bf16[32,1024]{1,0:T(8,128)(2,1)}, u32[]{:S(2)}) copy-start(bf16[32,1024]{1,0:T(8,128)(2,1)} %points.3) | copy-start | bytes 196612
  10.4 6.3 %collective-permute-start.2 = (bf16[4,64,128]{2,1,0:T(8,128)(2,1)S(1)}, bf16[4,64,128]{2,1,0:T(8,128)(2,1)S(1)}, u32[]{:S(2)}, u32[]{:S(2)}) collective-permute-start(bf16[4,64,128]{2,1,0:T(8,128)(2,1)S(1)} %shard_map.95), channel_id=1, source_target_pairs={{0,4},{4,0},{8,12},{12,8},{16,20},{20,16},{24,28},{28,24},{1,5},{5... | collective-permute-start | bytes 196616 | tf_op jit(solution)/shard_map/ppermute | solution.py:274
  10.7 3.8 %collective-permute-start.3 = (bf16[2,32,128]{2,1,0:T(8,128)(2,1)S(1)}, bf16[2,32,128]{2,1,0:T(8,128)(2,1)S(1)}, u32[]{:S(2)}, u32[]{:S(2)}) collective-permute-start(bf16[2,32,128]{2,1,0:T(8,128)(2,1)S(1)} %get-tuple-element.18), channel_id=1, source_target_pairs={{0,1},{1,0},{2,3},{3,2},{4,5},{5,4},{6,7},{7,6},{8,9},{9,8},{10,11... | collective-permute-start | bytes 49160 | tf_op jit(solution)/shard_map/ppermute | solution.py:285
  12.4 3.7 %collective-permute-start.4 = (bf16[2,32,128]{2,1,0:T(8,128)(2,1)S(1)}, bf16[2,32,128]{2,1,0:T(8,128)(2,1)S(1)}, u32[]{:S(2)}, u32[]{:S(2)}) collective-permute-start(bf16[2,32,128]{2,1,0:T(8,128)(2,1)S(1)} %get-tuple-element.20), channel_id=1, source_target_pairs={{0,4},{1,2},{2,1},{3,7},{4,0},{5,6},{6,5},{7,3},{8,12},{9,10},{10,... | collective-permute-start | bytes 49160 | tf_op jit(solution)/shard_map/ppermute | solution.py:285
